TPU v7x, 8 devices: a whole 2x2x1 slice. The times are simulated.
8 devices in a mesh: dp: 2 (over z, y), cp: 4 (over x, core).
Axes of the slice: x: 2, y: 2, z: 1, core: 2. Of those that a mesh axis runs over, the one named last changes fastest.
Arguments:
- x_in: bfloat16 [2048, 1536], P(('dp', 'cp')), parts along dimension 0
- dy_in: bfloat16 [2048, 1536], P(('dp', 'cp')), parts along dimension 0
- w_q: bfloat16 [1536, 1536], replicated
- w_k: bfloat16 [1536, 256], replicated
- w_v: bfloat16 [1536, 256], replicated
- w_o: bfloat16 [1536, 1536], replicated
Outputs:
- output 1: bfloat16 [2048, 1536], P(('dp', 'cp')), parts along dimension 0
- output 2: bfloat16 [2048, 1536], P(('dp', 'cp')), parts along dimension 0
There are 2 independent parts. A program takes and returns all parts, laid end to end along the dimension named above; an argument that names none is the same for every part.
All inputs are finite; a program needn't handle non-finite values.
Results may differ from a plain program's by a relative error of at most 0.0108757.
Values are sent between devices in bfloat16 or wider.
A program may use at most 1 GiB of HBM per device.

v0:
```python
import jax
import jax.numpy as jnp
from jax import lax
from jax.sharding import PartitionSpec as P

HEAD_DIM = 128
SCORE_LIMIT = 8388608


def block_rows(n_rows, n_heads, n_keys):
    blk_rows = n_rows
    for step_idx in range(30):
        if blk_rows % 2 == 0 and blk_rows > 8 and blk_rows * n_heads * n_keys > SCORE_LIMIT:
            blk_rows = blk_rows // 2
    return blk_rows


def split_rows(array_in, blk_rows):
    return array_in.reshape((array_in.shape[0] // blk_rows, blk_rows) + array_in.shape[1:])


def project(rows_in, weight):
    return jnp.dot(rows_in, weight, preferred_element_type=jnp.float32).astype(jnp.bfloat16)


def attend_forward(q_loc, k_all, v_all, blk_rows):
    n_rows, kv_heads, q_group, head_dim = q_loc.shape
    score_scale = head_dim ** -0.5

    def one_block(q_blk):
        scores = jnp.einsum("thjd,uhd->thju", q_blk, k_all, preferred_element_type=jnp.float32) * score_scale
        lse_blk = jax.nn.logsumexp(scores, axis=-1, keepdims=True)
        prob_bf = jnp.exp(scores - lse_blk).astype(jnp.bfloat16)
        out_blk = jnp.einsum("thju,uhd->thjd", prob_bf, v_all, preferred_element_type=jnp.float32).astype(jnp.bfloat16)
        return out_blk, lse_blk

    out_blocks, lse_blocks = lax.map(one_block, split_rows(q_loc, blk_rows))
    return out_blocks.reshape(n_rows, kv_heads, q_group, head_dim), lse_blocks.reshape(n_rows, kv_heads, q_group, 1)


def attend_backward(q_loc, k_all, v_all, lse_loc, delta_loc, do_loc, blk_rows):
    n_rows, kv_heads, q_group, head_dim = q_loc.shape
    score_scale = head_dim ** -0.5

    def one_block(acc_pair, block_in):
        dk_acc, dv_acc = acc_pair
        q_blk, do_blk, lse_blk, delta_blk = block_in
        scores = jnp.einsum("thjd,uhd->thju", q_blk, k_all, preferred_element_type=jnp.float32) * score_scale
        prob_bf = jnp.exp(scores - lse_blk).astype(jnp.bfloat16)
        dprob = jnp.einsum("thjd,uhd->thju", do_blk, v_all, preferred_element_type=jnp.float32)
        dscore = (prob_bf.astype(jnp.float32) * (dprob - delta_blk)).astype(jnp.bfloat16)
        dq_blk = (jnp.einsum("thju,uhd->thjd", dscore, k_all, preferred_element_type=jnp.float32) * score_scale).astype(jnp.bfloat16)
        dk_acc = dk_acc + jnp.einsum("thju,thjd->uhd", dscore, q_blk, preferred_element_type=jnp.float32) * score_scale
        dv_acc = dv_acc + jnp.einsum("thju,thjd->uhd", prob_bf, do_blk, preferred_element_type=jnp.float32)
        return (dk_acc, dv_acc), dq_blk

    zero_acc = jnp.zeros(k_all.shape, jnp.float32)
    blocks_in = (split_rows(q_loc, blk_rows), split_rows(do_loc, blk_rows), split_rows(lse_loc, blk_rows), split_rows(delta_loc, blk_rows))
    acc_final, dq_blocks = lax.scan(one_block, (zero_acc, zero_acc), blocks_in)
    return dq_blocks.reshape(n_rows, kv_heads * q_group * head_dim), acc_final[0], acc_final[1]


def solution(mesh):
    n_group = mesh.shape["cp"]
    row_spec = P(("dp", "cp"), None)
    full_spec = P(None, None)

    def local_body(x_loc, dy_loc, w_q, w_k, w_v, w_o):
        n_rows = x_loc.shape[0]
        q_heads = w_q.shape[1] // HEAD_DIM
        kv_heads = w_k.shape[1] // HEAD_DIM
        q_group = q_heads // kv_heads
        blk_rows = block_rows(n_rows, q_heads, n_rows * n_group)
        q_loc = project(x_loc, w_q).reshape(n_rows, kv_heads, q_group, HEAD_DIM)
        k_loc = project(x_loc, w_k).reshape(n_rows, kv_heads, HEAD_DIM)
        v_loc = project(x_loc, w_v).reshape(n_rows, kv_heads, HEAD_DIM)
        k_all = lax.all_gather(k_loc, "cp", axis=0, tiled=True)
        v_all = lax.all_gather(v_loc, "cp", axis=0, tiled=True)
        out_loc, lse_loc = attend_forward(q_loc, k_all, v_all, blk_rows)
        y_loc = project(out_loc.reshape(n_rows, q_heads * HEAD_DIM), w_o)
        do_loc = jnp.einsum("te,ce->tc", dy_loc, w_o, preferred_element_type=jnp.float32).astype(jnp.bfloat16).reshape(n_rows, kv_heads, q_group, HEAD_DIM)
        delta_loc = jnp.einsum("thjd,thjd->thj", do_loc, out_loc, preferred_element_type=jnp.float32)[..., None]
        dq_flat, dk_part, dv_part = attend_backward(q_loc, k_all, v_all, lse_loc, delta_loc, do_loc, blk_rows)
        dk_own = lax.psum_scatter(dk_part, "cp", scatter_dimension=0, tiled=True).astype(jnp.bfloat16).reshape(n_rows, kv_heads * HEAD_DIM)
        dv_own = lax.psum_scatter(dv_part, "cp", scatter_dimension=0, tiled=True).astype(jnp.bfloat16).reshape(n_rows, kv_heads * HEAD_DIM)
        dx_acc = (jnp.einsum("tc,ec->te", dq_flat, w_q, preferred_element_type=jnp.float32)
                  + jnp.einsum("tc,ec->te", dk_own, w_k, preferred_element_type=jnp.float32)
                  + jnp.einsum("tc,ec->te", dv_own, w_v, preferred_element_type=jnp.float32))
        return y_loc, dx_acc.astype(jnp.bfloat16)

    return jax.shard_map(local_body, mesh=mesh,
                         in_specs=(row_spec, row_spec, full_spec, full_spec, full_spec, full_spec),
                         out_specs=(row_spec, row_spec), check_vma=False)
```

profile of v0, /device:TPU:0, one launch (start us, length us, event | category | flops | bytes accessed | tf_op | source)
XLA Modules:
  0.0 121.5 jit_solution(9536257550906322196)
XLA Ops:
  7.2 0.0 reduce-scatter.3.cloned.1.call-start
  7.2 1.1 copy-done
  8.3 3.7 %convolution_convert_fusion.2 = bf16[256,1536]{1,0:T(8,128)(2,1)S(1)} fusion(bf16[256,1536]{1,0:T(8,128)(2,1)S(1)} %copy-done, bf16[1536,1536]{1,0:T(8,128)(2,1)} %param.8), kind=kOutput, calls=%fused_computation.15 | convolution fusion | flops 1208352768 | bytes 6291456 | tf_op jit(solution)/shard_map/dot_general | solution.py:23
  12.0 0.3 copy.20
  12.3 0.4 convolution_convert_fusion.4
  12.8 0.1 copy.19
  12.9 11.9 %all_gather.7 = bf16[1024,2,128]{2,0,1:T(8,128)(2,1)S(1)} all-gather(bf16[256,2,128]{2,0,1:T(8,128)(2,1)S(1)} %copy.19), channel_id=1, replica_groups=mesh['dp'=2,'cp'=4] {'cp'}, dimensions={0}, use_global_device_ids=true | all-gather | bytes 655360 | tf_op jit(solution)/shard_map/all_gather | solution.py:77
  24.7 1.8 %bitcast_reduce_fusion = (f32[256,2,6]{0,2,1:T(8,128)S(1)}, f32[2,1024,256,6]{2,1,3,0:T(8,128)S(1)}) fusion(bf16[256,2,6,128]{0,3,2,1:T(8,128)(2,1)S(1)} %bitcast.99, bf16[1024,2,128]{2,0,1:T(8,128)(2,1)S(1)} %all_gather.7), kind=kOutput, calls=%fused_computation.5 | convolution fusion | flops 811594752 | bytes 13905920 | tf_op jit(solution)/shard_map/while/body/eval_jaxpr/thjd,uhd->thju/dot_general | solution.py:31
  26.6 2.1 %fusion.3 = f32[256,2,6]{0,2,1:T(8,128)S(1)} fusion(f32[2,1024,256,6]{2,1,3,0:T(8,128)S(1)} %get-tuple-element.31, f32[256,2,6]{0,2,1:T(8,128)S(1)} %is-finite_select_fusion), kind=kLoop, calls=%fused_computation.7 | loop fusion | flops 9434112 | bytes 12607488 | tf_op jit(solution)/shard_map/while/body/eval_jaxpr/reduce_sum | solution.py:32
  28.7 2.4 %copy-done.1 = f32[2,1024,256,6]{2,1,3,0:T(8,128)} copy-done((f32[2,1024,256,6]{2,1,3,0:T(8,128)}, f32[2,1024,256,6]{2,1,3,0:T(8,128)S(1)}, u32[]{:S(2)}) %copy-start.1) | copy-done | bytes 12582936
  31.1 9.3 %fusion.5 = bf16[256,2,6,1024]{0,3,2,1:T(8,128)(2,1)} fusion(f32[2,1024,256,6]{2,1,3,0:T(8,128)} %copy-done.1, f32[256,2,6]{0,2,1:T(8,128)S(1)} %log_add_fusion), kind=kLoop, calls=%fused_computation.9 | loop fusion | flops 9437184 | bytes 18886656 | tf_op jit(solution)/shard_map/while/body/eval_jaxpr/convert_element_type | solution.py:33
  40.4 4.6 %convolution_convert_fusion = bf16[256,1536]{1,0:T(8,128)(2,1)} fusion(bf16[256,1536]{1,0:T(8,128)(2,1)S(1)} %copy-done.10, bf16[1536,1536]{1,0:T(8,128)(2,1)} %param.11), kind=kOutput, calls=%fused_computation.13 | convolution fusion | flops 1208352768 | bytes 6291456 | tf_op jit(solution)/shard_map/te,ce->tc/dot_general | solution.py:81
  45.0 2.4 %copy.23 = bf16[256,1536]{0,1:T(8,128)(2,1)} copy(bf16[256,1536]{1,0:T(8,128)(2,1)} %convolution_convert_fusion) | data formatting | bytes 1572864 | tf_op jit(solution)/shard_map/convert_element_type | solution.py:81
  47.4 1.6 %convolution_convert_fusion.5 = bf16[256,256]{0,1:T(8,128)(2,1)S(1)} fusion(bf16[256,1536]{1,0:T(8,128)(2,1)S(1)} %copy-done, bf16[1536,256]{1,0:T(8,128)(2,1)} %param.10), kind=kOutput, calls=%fused_computation.25 | convolution fusion | flops 201392128 | bytes 1703936 | tf_op jit(solution)/shard_map/dot_general | solution.py:23
  49.1 9.3 %all_gather.6 = bf16[1024,2,128]{0,2,1:T(8,128)(2,1)S(1)} all-gather(bf16[256,2,128]{0,2,1:T(8,128)(2,1)S(1)} %bitcast.105), channel_id=1, replica_groups=mesh['dp'=2,'cp'=4] {'cp'}, dimensions={0}, use_global_device_ids=true | all-gather | bytes 655360 | tf_op jit(solution)/shard_map/all_gather | solution.py:78
  58.4 5.0 %fusion.7 = (f32[256,2,6]{0,2,1:T(8,128)S(1)}, bf16[2,128,256,6]{2,1,3,0:T(8,128)(2,1)}) fusion(bf16[256,2,6,128]{0,3,2,1:T(8,128)(2,1)} %bitcast.96, bf16[256,2,6,1024]{0,3,2,1:T(8,128)(2,1)} %fusion.5, bf16[1024,2,128]{0,2,1:T(8,128)(2,1)S(1)} %all_gather.6), kind=kOutput, calls=%fused_computation.17 | convolution fusion | flops 807269376 | bytes 8400896 | tf_op jit(solution)/shard_map/while/body/eval_jaxpr/thju,uhd->thjd/dot_general | solution.py:34
  63.4 1.9 %fusion.1 = bf16[256,2,6,1024]{0,3,2,1:T(8,128)(2,1)S(1)} fusion(bf16[256,2,6,1024]{0,3,2,1:T(8,128)(2,1)S(1)} %bitcast.95, f32[256,2,6]{0,2,1:T(8,128)S(1)} %get-tuple-element.32, bf16[256,2,6,128]{0,3,2,1:T(8,128)(2,1)S(1)} %bitcast.97, bf16[1024,2,128]{0,2,1:T(8,128)(2,1)S(1)} %all_gather.6), kind=kOutput, calls=%fused_computation.2 | convolution fusion | flops 817889280 | bytes 13905920 | tf_op jit(solution)/shard_map/while/body/eval_jaxpr/thjd,uhd->thju/dot_general | solution.py:50
  65.3 2.6 %copy-done.2 = bf16[256,2,6,1024]{0,3,2,1:T(8,128)(2,1)} copy-done((bf16[256,2,6,1024]{0,3,2,1:T(8,128)(2,1)}, bf16[256,2,6,1024]{0,3,2,1:T(8,128)(2,1)S(1)}, u32[]{:S(2)}) %copy-start.2) | copy-done | bytes 6291480
  67.9 3.2 %fusion.9 = f32[1024,2,128]{0,2,1:T(8,128)} fusion(bf16[256,2,6,128]{0,3,2,1:T(8,128)(2,1)S(1)} %bitcast.100, bf16[256,2,6,1024]{0,3,2,1:T(8,128)(2,1)S(1)} %fusion.1), kind=kOutput, calls=%fused_computation.23 | convolution fusion | flops 805568512 | bytes 8126464 | tf_op jit(solution)/shard_map/while/body/eval_jaxpr/thju,thjd->uhd/dot_general | solution.py:53
  71.1 0.0 reduce-scatter.3.cloned.1.call-update
  71.1 0.0 reduce-scatter.5.cloned.1.call-start
  71.2 5.9 %convolution_bitcast_fusion = f32[1024,2,128]{0,2,1:T(8,128)} fusion(bf16[256,2,6,128]{0,3,2,1:T(8,128)(2,1)S(1)} %bitcast.98, bf16[256,2,6,1024]{0,3,2,1:T(8,128)(2,1)} %fusion.5), kind=kOutput, calls=%fused_computation.20 | convolution fusion | flops 805306368 | bytes 8126464 | tf_op jit(solution)/shard_map/while/body/eval_jaxpr/thju,thjd->uhd/dot_general | solution.py:54
  77.1 0.0 reduce-scatter.5.cloned.1.call-update
  77.1 4.0 %multiply_convert_fusion = bf16[2,128,256,6]{2,1,3,0:T(8,128)(2,1)S(1)} fusion(bf16[256,2,6,1024]{0,3,2,1:T(8,128)(2,1)} %copy-done.2, bf16[1024,2,128]{2,0,1:T(8,128)(2,1)S(1)} %all_gather.7), kind=kOutput, calls=%fused_computation.18 | convolution fusion | flops 806092800 | bytes 7602176 | tf_op jit(solution)/shard_map/while/body/eval_jaxpr/thju,uhd->thjd/dot_general | solution.py:52
  81.1 5.0 %fusion.15 = f32[256,1536]{1,0:T(8,128)} fusion(bf16[256,1536]{0,1:T(8,128)(2,1)S(1)} %bitcast.102, bf16[1536,1536]{1,0:T(8,128)(2,1)} %param.8), kind=kOutput, calls=%fused_computation.33 | convolution fusion | flops 1207959552 | bytes 7077888 | tf_op jit(solution)/shard_map/tc,ec->te/dot_general | solution.py:86
  86.2 2.3 %convolution_convert_fusion.1 = bf16[256,1536]{1,0:T(8,128)(2,1)} fusion(bf16[256,1536]{0,1:T(8,128)(2,1)S(1)} %bitcast.101, bf16[1536,1536]{1,0:T(8,128)(2,1)S(1)} %bitcast.108), kind=kOutput, calls=%fused_computation.14 | convolution fusion | flops 1208352768 | bytes 6291456 | tf_op jit(solution)/shard_map/dot_general | solution.py:23
  88.5 2.3 %reduce-scatter.3.cloned.1.call-done = f32[256,2,128]{0,2,1:T(8,128)} async-done(((f32[1024,2,128]{0,2,1:T(8,128)}), f32[256,2,128]{0,2,1:T(8,128)}) %reduce-scatter.3.cloned.1.call-update) | async-done | bytes 262160 | tf_op jit(solution)/shard_map/reduce_scatter | solution.py:84
  90.7 1.0 convert_element_type.64
  91.7 2.1 %convolution_add_fusion.1 = f32[256,1536]{1,0:T(8,128)S(1)} fusion(f32[256,1536]{1,0:T(8,128)} %fusion.15, bf16[256,256]{0,1:T(8,128)(2,1)S(1)} %bitcast.103, bf16[1536,256]{1,0:T(8,128)(2,1)} %param.9), kind=kOutput, calls=%fused_computation.11 | convolution fusion | flops 201719808 | bytes 4063232 | tf_op jit(solution)/shard_map/tc,ec->te/dot_general | solution.py:87
  93.8 18.6 %reduce-scatter.5.cloned.1.call-done = f32[256,2,128]{0,2,1:T(8,128)} async-done(((f32[1024,2,128]{0,2,1:T(8,128)}), f32[256,2,128]{0,2,1:T(8,128)}) %reduce-scatter.5.cloned.1.call-update) | async-done | bytes 262160 | tf_op jit(solution)/shard_map/reduce_scatter | solution.py:85
  112.4 1.0 convert_element_type.65
  113.4 1.3 %fusion.6 = bf16[256,1536]{1,0:T(8,128)(2,1)} fusion(f32[256,1536]{1,0:T(8,128)S(1)} %convolution_add_fusion.1, bf16[256,256]{0,1:T(8,128)(2,1)S(1)} %bitcast.104, bf16[1536,256]{1,0:T(8,128)(2,1)S(1)} %copy-done.7), kind=kOutput, calls=%fused_computation.12 | convolution fusion | flops 202113024 | bytes 3276800 | tf_op jit(solution)/shard_map/tc,ec->te/dot_general | solution.py:88
  (31 shorter events, 0.1 us)
Async XLA Ops:
  7.2 1.1 copy-start
  7.2 5.1 %copy-start.8 = (bf16[1536,256]{1,0:T(8,128)(2,1)S(1)}, bf16[1536,256]{1,0:T(8,128)(2,1)}, u32[]{:S(2)}) copy-start(bf16[1536,256]{1,0:T(8,128)(2,1)} %param.9) | copy-start | bytes 2359300
  7.2 83.5 %reduce-scatter.3.cloned.1.call-start = ((), (), s32[]{:S(2)}) async-start(), calls=%async_computation.2 | async-start | bytes 1310720 | tf_op jit(solution)/shard_map/reduce_scatter | solution.py:84
  12.3 14.2 %copy-start.5 = (bf16[256,1536]{0,1:T(8,128)(2,1)}, bf16[256,1536]{0,1:T(8,128)(2,1)S(1)}, u32[]{:S(2)}) copy-start(bf16[256,1536]{0,1:T(8,128)(2,1)S(1)} %copy.20) | copy-start | bytes 2359300
  26.5 4.5 %copy-start.1 = (f32[2,1024,256,6]{2,1,3,0:T(8,128)}, f32[2,1024,256,6]{2,1,3,0:T(8,128)S(1)}, u32[]{:S(2)}) copy-start(f32[2,1024,256,6]{2,1,3,0:T(8,128)S(1)} %get-tuple-element.31) | copy-start | bytes 37748740
  31.1 9.3 %copy-start.10 = (bf16[256,1536]{1,0:T(8,128)(2,1)S(1)}, bf16[256,1536]{1,0:T(8,128)(2,1)}, u32[]{:S(2)}) copy-start(bf16[256,1536]{1,0:T(8,128)(2,1)} %param.7) | copy-start | bytes 2359300
  45.0 18.4 %slice-start = ((s8[6291456]{0:T(1024)(128)(4,1)}), s8[2097152]{0:T(1024)(128)(4,1)S(1)}, s32[]{:S(2)}) async-start(s8[6291456]{0:T(1024)(128)(4,1)} %bitcast.94), calls=%async_computation.4 | async-start | bytes 4194304
  47.4 16.0 %copy-start.3 = (bf16[256,1536]{0,1:T(8,128)(2,1)S(1)}, bf16[256,1536]{0,1:T(8,128)(2,1)}, u32[]{:S(2)}) copy-start(bf16[256,1536]{0,1:T(8,128)(2,1)} %copy.23) | copy-start | bytes 2359300
  58.4 5.0 %slice-start.1 = ((s8[6291456]{0:T(1024)(128)(4,1)}), s8[4194304]{0:T(1024)(128)(4,1)S(1)}, s32[]{:S(2)}) async-start(s8[6291456]{0:T(1024)(128)(4,1)} %bitcast.94), calls=%async_computation.5 | async-start | bytes 8388608
  63.4 4.5 %copy-start.6 = (bf16[256,1536]{0,1:T(8,128)(2,1)S(1)}, bf16[256,1536]{0,1:T(8,128)(2,1)}, u32[]{:S(2)}) copy-start(bf16[256,1536]{0,1:T(8,128)(2,1)} %copy-done.5) | copy-start | bytes 2359300
  65.3 2.7 %copy-start.2 = (bf16[256,2,6,1024]{0,3,2,1:T(8,128)(2,1)}, bf16[256,2,6,1024]{0,3,2,1:T(8,128)(2,1)S(1)}, u32[]{:S(2)}) copy-start(bf16[256,2,6,1024]{0,3,2,1:T(8,128)(2,1)S(1)} %fusion.1) | copy-start | bytes 18874372
  67.9 3.2 %copy-start.4 = (bf16[256,1536]{0,1:T(8,128)(2,1)S(1)}, bf16[256,1536]{0,1:T(8,128)(2,1)}, u32[]{:S(2)}) copy-start(bf16[256,1536]{0,1:T(8,128)(2,1)} %copy.23) | copy-start | bytes 2359300
  71.1 41.3 %reduce-scatter.5.cloned.1.call-start = ((), (), s32[]{:S(2)}) async-start(), calls=%async_computation.3 | async-start | bytes 1310720 | tf_op jit(solution)/shard_map/reduce_scatter | solution.py:85
  77.1 9.0 %copy-start.9 = (bf16[2,128,256,6]{2,1,3,0:T(8,128)(2,1)S(1)}, bf16[2,128,256,6]{2,1,3,0:T(8,128)(2,1)}, u32[]{:S(2)}) copy-start(bf16[2,128,256,6]{2,1,3,0:T(8,128)(2,1)} %get-tuple-element.33) | copy-start | bytes 2359300
  77.1 9.0 %slice-start.2 = ((s8[4718592]{0:T(1024)(128)(4,1)}), s8[4194304]{0:T(1024)(128)(4,1)S(1)}, s32[]{:S(2)}) async-start(s8[4718592]{0:T(1024)(128)(4,1)} %bitcast.107), calls=%async_computation.6 | async-start | bytes 8388608
  81.1 5.0 %slice-start.3 = ((s8[4718592]{0:T(1024)(128)(4,1)}), s8[524288]{0:T(1024)(128)(4,1)S(1)}, s32[]{:S(2)}) async-start(s8[4718592]{0:T(1024)(128)(4,1)} %bitcast.107), calls=%async_computation.7 | async-start | bytes 1048576
  86.2 27.2 %copy-start.7 = (bf16[1536,256]{1,0:T(8,128)(2,1)S(1)}, bf16[1536,256]{1,0:T(8,128)(2,1)}, u32[]{:S(2)}) copy-start(bf16[1536,256]{1,0:T(8,128)(2,1)} %param.10) | copy-start | bytes 2359300
Sparse Core Ops, SparseCore 0:
  71.3 19.4 reduce-scatter.2
  93.2 19.1 reduce-scatter.4
where the time goes:
time: 122 us
  matrix products  42.8 us (35%)
  blocking collectives  21.2 us (17%)
  waiting for transfers between devices  20.9 us (17%)
  between operations  14.3 us (12%)
  other arithmetic  13.3 us (11%)
  local copies, waits for them, and re-layouts  8.98 us (7%)
    reduce_scatter x1, waiting for transfers between devices, local_body(): lax.psum_scatter(dv_part, 'cp', scatter_dimension=0, tiled=True)  18.6 us
    all_gather x1, blocking collectives, local_body(): k_all = lax.all_gather(k_loc, 'cp', axis=0, tiled=True)  11.9 us
    all_gather x1, blocking collectives, local_body(): v_all = lax.all_gather(v_loc, 'cp', axis=0, tiled=True)  9.32 us
    convert_element_type x1, other arithmetic, one_block(): prob_bf = jnp.exp(scores - lse_blk).astype(jnp.bfloat16)  9.26 us
    dot_general x4, matrix products, project(): jnp.dot(rows_in, weight, preferred_element_type=jnp.float32)  8.05 us
    unnamed x30, local copies, waits for them, and re-layouts  6.16 us
    dot_general x1, matrix products, one_block(): jnp.einsum('thju,thjd->uhd', prob_bf, do_blk, preferred_element_type=jnp....  5.88 us
    dot_general x1, matrix products, local_body(): jnp.einsum('tc,ec->te', dq_flat, w_q, preferred_element_type=jnp.float32)  5.01 us
  transfers between devices with their start and end apart: 2, of which 2 were waited for; matrix products, arithmetic and copies ran while one was open for 17% of the time, Pallas kernels for 0%

commit v1 on v0

v1 whole, which is shorter than its diff:
```python
import functools
import math

import jax
import jax.numpy as jnp
from jax import lax
from jax.experimental import pallas as pl
from jax.experimental.pallas import tpu as pltpu
from jax.sharding import PartitionSpec as P

HEAD_DIM = 128
MESH = pl.DeviceIdType.MESH
F32 = jnp.float32
BF16 = jnp.bfloat16
NT = (((1,), (1,)), ((), ()))
NN = (((1,), (0,)), ((), ()))


def mm(a, b, dims=NN):
    return lax.dot_general(a, b, dims, preferred_element_type=F32)


def kernel(rows, d_model, q_heads, kv_heads,
           x_hbm, dy_hbm, wq_hbm, wk_hbm, wv_hbm, wo_hbm,
           y_hbm, dx_hbm,
           x_v, dy_v, wq_v, wk_v, wv_v, wo_v,
           qs, dot_v, k_all, v_all, kt, vt, pt, ds_t, s_buf, o_v, ot_v, dq_v,
           part, recv_a, recv_b, recv_c, send_c, dx_acc, y_v, dx_v,
           in_sem, out_sem, ag_send, ag_recv, rs_send, rs_recv):
    group = q_heads // kv_heads
    d = HEAD_DIM
    n_keys = 4 * rows
    half = group * rows
    scale = d ** -0.5
    gain = scale * math.log2(math.e)

    me = lax.axis_index("cp")
    core = lax.rem(me, 2)
    partner = me + 1 - 2 * core
    cross = lax.rem(me + 2, 4)

    barrier = pltpu.get_barrier_semaphore()
    for peer in (partner, cross):
        pl.semaphore_signal(barrier, inc=1, device_id={"cp": peer}, device_id_type=MESH)

    qcols = q_heads * d // 2
    loads = [
        pltpu.make_async_copy(x_hbm, x_v, in_sem.at[0]),
        pltpu.make_async_copy(wk_hbm, wk_v, in_sem.at[1]),
        pltpu.make_async_copy(wv_hbm, wv_v, in_sem.at[2]),
        pltpu.make_async_copy(wq_hbm.at[:, :qcols], wq_v.at[:, :qcols], in_sem.at[3]),
        pltpu.make_async_copy(wq_hbm.at[:, qcols:], wq_v.at[:, qcols:], in_sem.at[4]),
        pltpu.make_async_copy(dy_hbm, dy_v, in_sem.at[5]),
        pltpu.make_async_copy(wo_hbm.at[:qcols], wo_v.at[:qcols], in_sem.at[6]),
        pltpu.make_async_copy(wo_hbm.at[qcols:], wo_v.at[qcols:], in_sem.at[7]),
    ]
    for copy in loads:
        copy.start()

    def item(i):
        return (k_all if i % 2 == 0 else v_all).at[i // 2]

    def slot(i, s):
        return item(i).at[pl.ds(s * rows, rows)]

    def ag_copy(i, hop):
        src, dst, peer = ((0, 1, partner), (0, 2, cross), (2, 3, partner))[hop]
        return pltpu.make_async_remote_copy(
            src_ref=slot(i, src), dst_ref=slot(i, dst),
            send_sem=ag_send.at[i, hop], recv_sem=ag_recv.at[i, hop],
            device_id={"cp": peer}, device_id_type=MESH)

    def forward(i):
        ag_copy(i, 1).wait_recv()
        ag_copy(i, 2).start()

    def finish_item(i):
        ag_copy(i, 0).wait_recv()
        ag_copy(i, 2).wait_recv()
        (kt if i % 2 == 0 else vt)[i // 2] = item(i)[...].T

    loads[0].wait()
    for w, copy, kv_ref in ((wk_v, loads[1], k_all), (wv_v, loads[2], v_all)):
        copy.wait()
        out = mm(x_v[...], w[...]).astype(BF16)
        for h in range(kv_heads):
            kv_ref[h, :rows, :] = out[:, h * d:(h + 1) * d]
    pl.semaphore_wait(barrier, 2)
    for i in range(2 * kv_heads):
        ag_copy(i, 1).start()
        ag_copy(i, 0).start()

    for n in range(q_heads // 2):
        if n == 0:
            loads[3].wait()
        if n == q_heads // 4:
            loads[4].wait()
        out = mm(x_v[...], wq_v[:, n * 2 * d:(n + 1) * 2 * d]).astype(BF16)
        for t in range(2):
            head = 2 * n + t
            h, j = head // group, head % group
            qs[h, j * rows:(j + 1) * rows, :] = out[:, t * d:(t + 1) * d]

    loads[5].wait()
    for n in range(q_heads // 2):
        if n == 0:
            loads[6].wait()
        if n == q_heads // 4:
            forward(0)
            loads[7].wait()
        out = mm(wo_v[n * 2 * d:(n + 1) * 2 * d, :], dy_v[...], NT).astype(BF16)
        for t in range(2):
            head = 2 * n + t
            h, j = head // group, head % group
            dot_v[h, :, j * rows:(j + 1) * rows] = out[t * d:(t + 1) * d, :]

    def probs(h, j):
        cols = pl.ds(pl.multiple_of(j * rows, rows), rows)
        q = qs[h, cols, :]
        m8 = None
        for c in range(4):
            s = mm(k_all[h, c * rows:(c + 1) * rows, :], q, NT)
            s_buf[c * rows:(c + 1) * rows, :] = s
            t8 = jnp.max(s.reshape(rows // 8, 8, rows), axis=0)
            m8 = t8 if m8 is None else jnp.maximum(m8, t8)
        mk = jnp.max(m8, axis=0, keepdims=True) * gain
        l8 = jnp.zeros((8, rows), F32)
        for c in range(4):
            e = jnp.exp2(s_buf[c * rows:(c + 1) * rows, :] * gain - mk)
            s_buf[c * rows:(c + 1) * rows, :] = e
            l8 = l8 + jnp.sum(e.reshape(rows // 8, 8, rows), axis=0)
        inv = 1.0 / jnp.sum(l8, axis=0, keepdims=True)
        for c in range(4):
            pt[h, c * rows:(c + 1) * rows, cols] = (s_buf[c * rows:(c + 1) * rows, :] * inv).astype(BF16)

    def outs(h, j):
        cols = pl.ds(pl.multiple_of(j * rows, rows), rows)
        head = pl.ds(pl.multiple_of((h * group + j) * d, d), d)
        o_t = mm(vt[h], pt[h, :, cols]).astype(BF16)
        o_v[:, head] = o_t.T
        do_t = dot_v[h, :, cols]
        delta = jnp.sum(do_t.astype(F32) * o_t.astype(F32), axis=0, keepdims=True)
        for c in range(4):
            dp = mm(v_all[h, c * rows:(c + 1) * rows, :], do_t)
            p = pt[h, c * rows:(c + 1) * rows, cols].astype(F32)
            ds_t[h, c * rows:(c + 1) * rows, cols] = (p * (dp - delta)).astype(BF16)

    def dqs(h, j):
        cols = pl.ds(pl.multiple_of(j * rows, rows), rows)
        head = pl.ds(pl.multiple_of((h * group + j) * d, d), d)
        dq_t = (mm(kt[h], ds_t[h, :, cols]) * scale).astype(BF16)
        dq_v[:, head] = dq_t.T

    def grads(r, s):
        h = r % kv_heads
        block = slice(s * rows, (s + 1) * rows)
        if r < kv_heads:
            return mm(pt[h, block, :], dot_v[h], NT)
        return mm(ds_t[h, block, :], qs[h])

    def rs_copy(r, kind):
        src, dst_ref, peer = ((part.at[r, 3], recv_a.at[r], partner),
                              (part.at[r, 1], recv_b.at[r], partner),
                              (send_c.at[r], recv_c.at[r], cross))[kind]
        return pltpu.make_async_remote_copy(
            src_ref=src, dst_ref=dst_ref,
            send_sem=rs_send.at[r, kind], recv_sem=rs_recv.at[r, kind],
            device_id={"cp": peer}, device_id_type=MESH)

    def reduce_first(r):
        part[r, 3] = grads(r, 3)
        rs_copy(r, 0).start()
        part[r, 2] = grads(r, 2)

    def reduce_cross(r):
        rs_copy(r, 0).wait_recv()
        send_c[r] = part[r, 2] + recv_a[r]
        rs_copy(r, 2).start()

    def reduce_local(r):
        part[r, 1] = grads(r, 1)
        rs_copy(r, 1).start()
        part[r, 0] = grads(r, 0)

    def loop(body, h, lo, hi):
        def step(j, carry):
            body(h, j)
            return carry
        lax.fori_loop(lo, hi, step, 0)

    finish_item(0)
    loop(probs, 0, 0, 3)
    forward(1)
    loop(probs, 0, 3, 6)
    forward(2)
    reduce_first(0)
    finish_item(1)
    finish_item(2)
    loop(probs, 1, 0, 3)
    reduce_cross(0)
    forward(3)
    loop(probs, 1, 3, 6)
    reduce_first(1)
    finish_item(3)
    loop(outs, 0, 0, 3)
    reduce_cross(1)
    loop(outs, 0, 3, 6)
    reduce_first(2)
    loop(outs, 1, 0, 3)
    reduce_cross(2)
    loop(outs, 1, 3, 6)
    reduce_first(3)
    reduce_local(0)
    reduce_cross(3)
    for r in range(1, 2 * kv_heads):
        reduce_local(r)
    for h in range(kv_heads):
        loop(dqs, h, 0, group)

    y_copies = []
    for n in range(d_model // 256):
        cols = slice(n * 256, (n + 1) * 256)
        y_v[:, cols] = mm(o_v[...], wo_v[:, cols]).astype(BF16)
        copy = pltpu.make_async_copy(y_v.at[:, cols], y_hbm.at[:, cols], out_sem.at[n])
        copy.start()
        y_copies.append(copy)
    for n in range(d_model // 256):
        cols = slice(n * 256, (n + 1) * 256)
        dx_acc[:, cols] = mm(dq_v[...], wq_v[cols, :], NT)

    own = []
    for r in range(2 * kv_heads):
        rs_copy(r, 1).wait_recv()
        rs_copy(r, 2).wait_recv()
        total = part[r, 0] + recv_b[r] + recv_c[r]
        if r >= kv_heads:
            total = total * scale
        own.append(total.astype(BF16))
    dv = jnp.concatenate(own[:kv_heads], axis=1)
    dk = jnp.concatenate(own[kv_heads:], axis=1)
    dx_copies = []
    for n in range(d_model // 256):
        cols = slice(n * 256, (n + 1) * 256)
        total = dx_acc[:, cols] + mm(dk, wk_v[cols, :], NT) + mm(dv, wv_v[cols, :], NT)
        dx_v[:, cols] = total.astype(BF16)
        copy = pltpu.make_async_copy(dx_v.at[:, cols], dx_hbm.at[:, cols], out_sem.at[6 + n])
        copy.start()
        dx_copies.append(copy)

    for i in range(2 * kv_heads):
        for hop in range(3):
            ag_copy(i, hop).wait_send()
    for r in range(2 * kv_heads):
        for kind in range(3):
            rs_copy(r, kind).wait_send()
    for copy in y_copies + dx_copies:
        copy.wait()


def solution(mesh):
    row_spec = P(("dp", "cp"), None)
    full_spec = P(None, None)

    def local_body(x_loc, dy_loc, w_q, w_k, w_v, w_o):
        rows, d_model = x_loc.shape
        d = HEAD_DIM
        q_heads = w_q.shape[1] // d
        kv_heads = w_k.shape[1] // d
        group = q_heads // kv_heads
        n_keys = 4 * rows
        qw = q_heads * d
        any_spec = pl.BlockSpec(memory_space=pl.ANY)
        out = jax.ShapeDtypeStruct((rows, d_model), BF16)
        items = 2 * kv_heads
        return pl.pallas_call(
            functools.partial(kernel, rows, d_model, q_heads, kv_heads),
            out_shape=(out, out),
            in_specs=[any_spec] * 6,
            out_specs=(any_spec, any_spec),
            scratch_shapes=[
                pltpu.VMEM((rows, d_model), BF16),
                pltpu.VMEM((rows, d_model), BF16),
                pltpu.VMEM((d_model, qw), BF16),
                pltpu.VMEM((d_model, kv_heads * d), BF16),
                pltpu.VMEM((d_model, kv_heads * d), BF16),
                pltpu.VMEM((qw, d_model), BF16),
                pltpu.VMEM((kv_heads, group * rows, d), BF16),
                pltpu.VMEM((kv_heads, d, group * rows), BF16),
                pltpu.VMEM((kv_heads, n_keys, d), BF16),
                pltpu.VMEM((kv_heads, n_keys, d), BF16),
                pltpu.VMEM((kv_heads, d, n_keys), BF16),
                pltpu.VMEM((kv_heads, d, n_keys), BF16),
                pltpu.VMEM((kv_heads, n_keys, group * rows), BF16),
                pltpu.VMEM((kv_heads, n_keys, group * rows), BF16),
                pltpu.VMEM((n_keys, rows), F32),
                pltpu.VMEM((rows, qw), BF16),
                pltpu.VMEM((q_heads, d, rows), BF16),
                pltpu.VMEM((rows, qw), BF16),
                pltpu.VMEM((items, 4, rows, d), F32),
                pltpu.VMEM((items, rows, d), F32),
                pltpu.VMEM((items, rows, d), F32),
                pltpu.VMEM((items, rows, d), F32),
                pltpu.VMEM((items, rows, d), F32),
                pltpu.VMEM((rows, d_model), F32),
                pltpu.VMEM((rows, d_model), BF16),
                pltpu.VMEM((rows, d_model), BF16),
                pltpu.SemaphoreType.DMA((8,)),
                pltpu.SemaphoreType.DMA((12,)),
                pltpu.SemaphoreType.DMA((items, 3)),
                pltpu.SemaphoreType.DMA((items, 3)),
                pltpu.SemaphoreType.DMA((items, 3)),
                pltpu.SemaphoreType.DMA((items, 3)),
            ],
            compiler_params=pltpu.CompilerParams(
                collective_id=0, has_side_effects=True,
                vmem_limit_bytes=60 * 1024 * 1024),
        )(x_loc, dy_loc, w_q, w_k, w_v, w_o)

    return jax.shard_map(local_body, mesh=mesh,
                         in_specs=(row_spec, row_spec, full_spec, full_spec, full_spec, full_spec),
                         out_specs=(row_spec, row_spec), check_vma=False)
```

time: 122 us -> 43 us (0.35)
  matrix products: 42.8 us -> 0 us
  Pallas kernels: 0 us -> 38.1 us
  blocking collectives: 21.2 us -> 0 us
  waiting for transfers between devices: 20.9 us -> 0 us
  between operations: 14.3 us -> 0.64 us
  other arithmetic: 13.3 us -> 0 us
  local copies, waits for them, and re-layouts: 8.98 us -> 4.13 us
    dot_general x14 -> x0, matrix products: 42.8 us -> none  [the longest x4 8.05 us: project(): jnp.dot(rows_in, weight, preferred_element_type=jnp.float32)]
    pallas_call x0 -> x1, Pallas kernels: none -> 38.1 us  [local_body(): pl.pallas_call(functools.partial(kernel, rows, d_model, q_heads, kv_heads...]
    all_gather x2 -> x0, blocking collectives: 21.2 us -> none  [the longest x1 11.9 us: local_body(): k_all = lax.all_gather(k_loc, 'cp', axis=0, tiled=True)]
    reduce_scatter x2 -> x0, waiting for transfers between devices: 20.9 us -> none  [the longest x1 18.6 us: local_body(): lax.psum_scatter(dv_part, 'cp', scatter_dimension=0, tiled=True)]
    convert_element_type x3 -> x0, other arithmetic: 11.2 us -> none  [the longest x1 9.26 us: one_block(): prob_bf = jnp.exp(scores - lse_blk).astype(jnp.bfloat16)]
    convert_element_type x2 -> x0, local copies, waits for them, and re-layouts: 2.71 us -> none  [the longest x1 2.43 us: local_body(): jnp.einsum('te,ce->tc', dy_loc, w_o, preferred_element_type=jnp.float32)]
    reduce_sum x1 -> x0, other arithmetic: 2.13 us -> none  [one_block(): lse_blk = jax.nn.logsumexp(scores, axis=-1, keepdims=True)]
    unnamed x30 -> x2, local copies, waits for them, and re-layouts: 6.16 us -> 4.13 us
  transfers between devices with their start and end apart: 2 -> 0, of which waited for: 2 -> 0; matrix products, arithmetic and copies ran while one was open for 17% -> 0% of each run, Pallas kernels for 0% -> 0%
where the time goes in v1:
time: 43 us; the launch traced here: 42.8 us
  Pallas kernels  38.1 us (89%)
  local copies, waits for them, and re-layouts  4.13 us (10%)
  between operations  0.64 us (1%)
    pallas_call x1, Pallas kernels, local_body(): pl.pallas_call(functools.partial(kernel, rows, d_model, q_heads, kv_heads...  38.1 us
    unnamed x2, local copies, waits for them, and re-layouts  4.13 us

profile of v1, /device:TPU:0, one launch (start us, length us, event | category | flops | bytes accessed | tf_op | source)
XLA Modules:
  0.0 42.8 jit_solution(17673746687292309533)
XLA Ops:
  0.6 38.1 %shard_map.77 = (bf16[256,1536]{1,0:T(8,128)(2,1)}, bf16[256,1536]{1,0:T(8,128)(2,1)}) custom-call(bf16[256,1536]{1,0:T(8,128)(2,1)} %x_hbm.1, bf16[256,1536]{1,0:T(8,128)(2,1)} %dy_hbm.1, bf16[1536,1536]{1,0:T(8,128)(2,1)} %wq_hbm.1, bf16[1536,256]{1,0:T(8,128)(2,1)} %wk_hbm.1, bf16[1536,256]{1,0:T(8,128)(2,1)} %wv_hbm.1, bf16[1536,1536]{1,0:T(8,128)(2,1)} %wo_hbm.1), custom_call_target="tpu_custom_call" | custom-call | tf_op jit(solution)/shard_map/pallas_call | solution.py:275
  38.7 2.1 %copy.10 = bf16[256,1536]{1,0:T(8,128)(2,1)} copy(bf16[256,1536]{1,0:T(8,128)(2,1)} %get-tuple-element.4) | data formatting | bytes 1572864
  40.8 2.1 %copy.11 = bf16[256,1536]{1,0:T(8,128)(2,1)} copy(bf16[256,1536]{1,0:T(8,128)(2,1)} %get-tuple-element.5) | data formatting | bytes 1572864

commit v2 on v1

v2 whole, which is shorter than its diff:
```python
import functools
import math

import jax
import jax.numpy as jnp
from jax import lax
from jax.experimental import pallas as pl
from jax.experimental.pallas import tpu as pltpu
from jax.sharding import PartitionSpec as P

HEAD_DIM = 128
CHUNK = 128
MESH = pl.DeviceIdType.MESH
F32 = jnp.float32
BF16 = jnp.bfloat16
NT = (((1,), (1,)), ((), ()))
NN = (((1,), (0,)), ((), ()))


def mm(a, b, dims=NN):
    return lax.dot_general(a, b, dims, preferred_element_type=F32)


def kernel(rows, d_model, q_heads, kv_heads,
           x_hbm, dy_hbm, wq_hbm, wk_hbm, wv_hbm, wo_hbm,
           y_v, dx_v,
           x_v, dy_v, wq_v, wk_v, wv_v, wo_v,
           qs, dot_v, k_all, v_all, kt, vt, pt, ds_t, e_buf, m_buf, l_buf, o_v, dq_v,
           part, recv_a, recv_b, recv_c, send_c, dx_acc,
           in_sem, ag_send, ag_recv, rs_send, rs_recv):
    group = q_heads // kv_heads
    d = HEAD_DIM
    n_keys = 4 * rows
    half = group * rows
    scale = d ** -0.5
    gain = scale * math.log2(math.e)

    me = lax.axis_index("cp")
    core = lax.rem(me, 2)
    partner = me + 1 - 2 * core
    cross = lax.rem(me + 2, 4)

    barrier = pltpu.get_barrier_semaphore()
    for peer in (partner, cross):
        pl.semaphore_signal(barrier, inc=1, device_id={"cp": peer}, device_id_type=MESH)

    qcols = q_heads * d // 2
    loads = [
        pltpu.make_async_copy(wk_hbm, wk_v, in_sem.at[1]),
        pltpu.make_async_copy(x_hbm, x_v, in_sem.at[0]),
        pltpu.make_async_copy(wv_hbm, wv_v, in_sem.at[2]),
        pltpu.make_async_copy(wq_hbm.at[:, :qcols], wq_v.at[:, :qcols], in_sem.at[3]),
        pltpu.make_async_copy(wq_hbm.at[:, qcols:], wq_v.at[:, qcols:], in_sem.at[4]),
        pltpu.make_async_copy(dy_hbm, dy_v, in_sem.at[5]),
        pltpu.make_async_copy(wo_hbm.at[:qcols], wo_v.at[:qcols], in_sem.at[6]),
        pltpu.make_async_copy(wo_hbm.at[qcols:], wo_v.at[qcols:], in_sem.at[7]),
    ]
    for copy in loads:
        copy.start()

    def item(i):
        return (k_all if i % 2 == 0 else v_all).at[i // 2]

    def slot(i, s):
        return item(i).at[pl.ds(s * rows, rows)]

    def ag_copy(i, hop):
        src, dst, peer = ((0, 1, partner), (0, 2, cross), (2, 3, partner))[hop]
        return pltpu.make_async_remote_copy(
            src_ref=slot(i, src), dst_ref=slot(i, dst),
            send_sem=ag_send.at[i, hop], recv_sem=ag_recv.at[i, hop],
            device_id={"cp": peer}, device_id_type=MESH)

    def forward(i):
        ag_copy(i, 1).wait_recv()
        ag_copy(i, 2).start()

    def transpose_item(i, ref):
        for s in range(4):
            ref[i // 2, :, s * rows:(s + 1) * rows] = slot(i, s)[...].T

    def head_of(i):
        h, j = i // group, i % group
        return h, slice(j * rows, (j + 1) * rows), slice(i * d, (i + 1) * d)

    def project_q(n):
        out = mm(x_v[...], wq_v[:, n * 2 * d:(n + 1) * 2 * d]).astype(BF16)
        for t in range(2):
            h, cols, _ = head_of(2 * n + t)
            qs[h, cols, :] = out[:, t * d:(t + 1) * d]

    def project_do(n):
        out = mm(wo_v[n * 2 * d:(n + 1) * 2 * d, :], dy_v[...], NT).astype(BF16)
        for t in range(2):
            h, cols, _ = head_of(2 * n + t)
            dot_v[h, :, cols] = out[t * d:(t + 1) * d, :]

    per_slot = rows // CHUNK

    def scores(i, s):
        h, cols, _ = head_of(i)
        j = i % group
        raw = mm(k_all[h, s * rows:(s + 1) * rows, :], qs[h, cols, :], NT)
        for c in range(per_slot):
            t = raw[c * CHUNK:(c + 1) * CHUNK] * gain
            t = t.reshape(CHUNK // 8, 8, rows)
            m8 = jnp.max(t, axis=0)
            e = jnp.exp2(t - m8[None])
            e_buf[j, s * rows + c * CHUNK:s * rows + (c + 1) * CHUNK, :] = e.reshape(CHUNK, rows)
            m_buf[j, s * per_slot + c] = m8
            l_buf[j, s * per_slot + c] = jnp.sum(e, axis=0)

    def finalize(i):
        h, cols, _ = head_of(i)
        j = i % group
        n_chunks = 4 * per_slot
        top = jnp.max(jnp.max(m_buf[j], axis=0), axis=0, keepdims=True)
        factor = [jnp.exp2(m_buf[j, c] - top) for c in range(n_chunks)]
        total = factor[0] * l_buf[j, 0]
        for c in range(1, n_chunks):
            total = total + factor[c] * l_buf[j, c]
        inv = 1.0 / jnp.sum(total, axis=0, keepdims=True)
        for c in range(n_chunks):
            f8 = factor[c] * inv
            e = e_buf[j, c * CHUNK:(c + 1) * CHUNK, :].reshape(CHUNK // 8, 8, rows)
            pt[h, c * CHUNK:(c + 1) * CHUNK, cols] = (e * f8[None]).reshape(CHUNK, rows).astype(BF16)

    def outs(i):
        h, cols, feats = head_of(i)
        o_t = mm(vt[h], pt[h, :, cols]).astype(BF16)
        o_v[:, feats] = o_t.T
        do_t = dot_v[h, :, cols]
        delta = jnp.sum(do_t.astype(F32) * o_t.astype(F32), axis=0, keepdims=True)
        for s in range(4):
            keys = slice(s * rows, (s + 1) * rows)
            dp = mm(v_all[h, keys, :], do_t)
            ds_t[h, keys, cols] = (pt[h, keys, cols].astype(F32) * (dp - delta)).astype(BF16)

    def dqs(i):
        h, cols, feats = head_of(i)
        dq_v[:, feats] = (mm(kt[h], ds_t[h, :, cols]) * scale).astype(BF16).T

    def grads(r, lo, hi):
        h = r % kv_heads
        block = slice(lo * rows, hi * rows)
        if r < kv_heads:
            out = mm(pt[h, block, :], dot_v[h], NT)
        else:
            out = mm(ds_t[h, block, :], qs[h])
        for s in range(lo, hi):
            part[r, s] = out[(s - lo) * rows:(s - lo + 1) * rows]

    def rs_copy(r, kind):
        src, dst, peer = ((part.at[r, 3], recv_a.at[r], partner),
                          (part.at[r, 1], recv_b.at[r], partner),
                          (send_c.at[r], recv_c.at[r], cross))[kind]
        return pltpu.make_async_remote_copy(
            src_ref=src, dst_ref=dst,
            send_sem=rs_send.at[r, kind], recv_sem=rs_recv.at[r, kind],
            device_id={"cp": peer}, device_id_type=MESH)

    def reduce_cross(r):
        rs_copy(r, 0).wait_recv()
        send_c[r] = part[r, 2] + recv_a[r]
        rs_copy(r, 2).start()

    first = range(group)
    second = range(group, q_heads)

    loads[0].wait()
    loads[1].wait()
    for w, copy, kv_ref in ((wk_v, None, k_all), (wv_v, loads[2], v_all)):
        if copy is not None:
            copy.wait()
        out = mm(x_v[...], w[...]).astype(BF16)
        for h in range(kv_heads):
            kv_ref[h, :rows, :] = out[:, h * d:(h + 1) * d]
        if copy is None:
            pl.semaphore_wait(barrier, 2)
        for h in range(kv_heads):
            i = 2 * h + (0 if copy is None else 1)
            ag_copy(i, 1).start()
            ag_copy(i, 0).start()

    loads[3].wait()
    for n in range(q_heads // 4):
        project_q(n)
    loads[4].wait()
    ag_copy(0, 0).wait_recv()
    for n in range(q_heads // 4):
        project_q(q_heads // 4 + n)
        for s in (0, 1):
            scores(n, s)
    loads[5].wait()
    loads[6].wait()
    for n in range(q_heads // 4):
        project_do(n)
        for s in (0, 1):
            scores(q_heads // 4 + n, s)
    loads[7].wait()
    forward(0)
    for n in range(q_heads // 4):
        project_do(q_heads // 4 + n)
        scores(2 * n, 2)
        scores(2 * n + 1, 2)
    ag_copy(0, 2).wait_recv()
    for i in first:
        scores(i, 3)
    for i in first:
        finalize(i)
    forward(1)
    grads(0, 3, 4)
    rs_copy(0, 0).start()
    grads(0, 2, 3)
    ag_copy(2, 0).wait_recv()
    for n in range(group):
        scores(group + n, 0)
        scores(group + n, 1)
        if n == 0:
            grads(0, 1, 2)
        if n == 2:
            grads(0, 0, 1)
    forward(2)
    reduce_cross(0)
    rs_copy(0, 1).start()
    ag_copy(1, 0).wait_recv()
    ag_copy(1, 2).wait_recv()
    transpose_item(1, vt)
    for i in first:
        outs(i)
        scores(group + i, 2)
    forward(3)
    ag_copy(2, 2).wait_recv()
    grads(2, 3, 4)
    for i in second:
        scores(i, 3)
    rs_copy(2, 0).start()
    grads(2, 2, 3)
    for i in second:
        finalize(i)
    grads(1, 3, 4)
    rs_copy(1, 0).start()
    grads(1, 2, 3)
    ag_copy(3, 0).wait_recv()
    ag_copy(3, 2).wait_recv()
    reduce_cross(2)
    transpose_item(3, vt)
    for i in range(group, group + group // 2):
        outs(i)
    reduce_cross(1)
    for i in range(group + group // 2, q_heads):
        outs(i)
    grads(3, 3, 4)
    rs_copy(3, 0).start()
    grads(3, 2, 3)
    for r in (2, 1):
        grads(r, 0, 2)
        rs_copy(r, 1).start()
    reduce_cross(3)
    grads(3, 0, 2)
    rs_copy(3, 1).start()
    transpose_item(0, kt)
    transpose_item(2, kt)
    for i in range(q_heads):
        dqs(i)
    for n in range(d_model // 256):
        cols = slice(n * 256, (n + 1) * 256)
        y_v[:, cols] = mm(o_v[...], wo_v[:, cols]).astype(BF16)
    for n in range(d_model // 256):
        cols = slice(n * 256, (n + 1) * 256)
        dx_acc[:, cols] = mm(dq_v[...], wq_v[cols, :], NT)

    def own(r):
        rs_copy(r, 1).wait_recv()
        rs_copy(r, 2).wait_recv()
        total = part[r, 0] + recv_b[r] + recv_c[r]
        if r >= kv_heads:
            total = total * scale
        return total.astype(BF16)

    for r in (0, 2, 1):
        g = own(r)
        h = r % kv_heads
        w = wv_v if r < kv_heads else wk_v
        for n in range(d_model // 256):
            cols = slice(n * 256, (n + 1) * 256)
            dx_acc[:, cols] += mm(g, w[cols, h * d:(h + 1) * d], NT)
    g = own(3)
    for n in range(d_model // 256):
        cols = slice(n * 256, (n + 1) * 256)
        total = dx_acc[:, cols] + mm(g, wk_v[cols, d:2 * d], NT)
        dx_v[:, cols] = total.astype(BF16)

    for i in range(2 * kv_heads):
        for hop in range(3):
            ag_copy(i, hop).wait_send()
    for r in range(2 * kv_heads):
        for kind in range(3):
            rs_copy(r, kind).wait_send()


def write_out(y_v, dx_v, y_hbm, dx_hbm, sem):
    copies = [pltpu.make_async_copy(y_v, y_hbm, sem.at[0]),
              pltpu.make_async_copy(dx_v, dx_hbm, sem.at[1])]
    for copy in copies:
        copy.start()
    for copy in copies:
        copy.wait()


def solution(mesh):
    row_spec = P(("dp", "cp"), None)
    full_spec = P(None, None)

    def local_body(x_loc, dy_loc, w_q, w_k, w_v, w_o):
        rows, d_model = x_loc.shape
        d = HEAD_DIM
        q_heads = w_q.shape[1] // d
        kv_heads = w_k.shape[1] // d
        group = q_heads // kv_heads
        n_keys = 4 * rows
        qw = q_heads * d
        hbm = pl.BlockSpec(memory_space=pltpu.HBM)
        vmem = pl.BlockSpec(memory_space=pltpu.VMEM)
        out = jax.ShapeDtypeStruct((rows, d_model), BF16)
        items = 2 * kv_heads
        y_v, dx_v = pl.pallas_call(
            functools.partial(kernel, rows, d_model, q_heads, kv_heads),
            out_shape=(out, out),
            in_specs=[hbm] * 6,
            out_specs=(vmem, vmem),
            scratch_shapes=[
                pltpu.VMEM((rows, d_model), BF16),
                pltpu.VMEM((rows, d_model), BF16),
                pltpu.VMEM((d_model, qw), BF16),
                pltpu.VMEM((d_model, kv_heads * d), BF16),
                pltpu.VMEM((d_model, kv_heads * d), BF16),
                pltpu.VMEM((qw, d_model), BF16),
                pltpu.VMEM((kv_heads, group * rows, d), BF16),
                pltpu.VMEM((kv_heads, d, group * rows), BF16),
                pltpu.VMEM((kv_heads, n_keys, d), BF16),
                pltpu.VMEM((kv_heads, n_keys, d), BF16),
                pltpu.VMEM((kv_heads, d, n_keys), BF16),
                pltpu.VMEM((kv_heads, d, n_keys), BF16),
                pltpu.VMEM((kv_heads, n_keys, group * rows), BF16),
                pltpu.VMEM((kv_heads, n_keys, group * rows), BF16),
                pltpu.VMEM((group, n_keys, rows), F32),
                pltpu.VMEM((group, n_keys // CHUNK, 8, rows), F32),
                pltpu.VMEM((group, n_keys // CHUNK, 8, rows), F32),
                pltpu.VMEM((rows, qw), BF16),
                pltpu.VMEM((rows, qw), BF16),
                pltpu.VMEM((items, 4, rows, d), F32),
                pltpu.VMEM((items, rows, d), F32),
                pltpu.VMEM((items, rows, d), F32),
                pltpu.VMEM((items, rows, d), F32),
                pltpu.VMEM((items, rows, d), F32),
                pltpu.VMEM((rows, d_model), F32),
                pltpu.SemaphoreType.DMA((8,)),
                pltpu.SemaphoreType.DMA((items, 3)),
                pltpu.SemaphoreType.DMA((items, 3)),
                pltpu.SemaphoreType.DMA((items, 3)),
                pltpu.SemaphoreType.DMA((items, 3)),
            ],
            compiler_params=pltpu.CompilerParams(
                collective_id=0, has_side_effects=True,
                vmem_limit_bytes=50 * 1024 * 1024),
        )(*(pltpu.with_memory_space_constraint(a, pltpu.HBM) for a in (x_loc, dy_loc, w_q, w_k, w_v, w_o)))
        return pl.pallas_call(
            write_out,
            out_shape=(out, out),
            in_specs=[pl.BlockSpec(memory_space=pl.ANY)] * 2,
            out_specs=(hbm, hbm),
            scratch_shapes=[pltpu.SemaphoreType.DMA((2,))],
            compiler_params=pltpu.CompilerParams(vmem_limit_bytes=4 * 1024 * 1024),
        )(y_v, dx_v)

    return jax.shard_map(local_body, mesh=mesh,
                         in_specs=(row_spec, row_spec, full_spec, full_spec, full_spec, full_spec),
                         out_specs=(row_spec, row_spec), check_vma=False)
```

time: 43 us -> 29.7 us (0.69)
  Pallas kernels: 38.1 us -> 28.8 us
  local copies, waits for them, and re-layouts: 4.13 us -> 0 us
    pallas_call x1, Pallas kernels: 38.1 us -> 27.6 us  [local_body(): pl.pallas_call(functools.partial(kernel, rows, d_model, q_heads, kv_heads...]
    unnamed x2 -> x0, local copies, waits for them, and re-layouts: 4.13 us -> none
    pallas_call x0 -> x1, Pallas kernels: none -> 1.16 us  [local_body(): pl.pallas_call(write_out, out_shape=(out, out), in_specs=[pl.BlockSpec(me...]
where the time goes in v2:
time: 29.7 us; the launch traced here: 29.6 us
  Pallas kernels  28.8 us (97%)
  between operations  0.8 us (3%)
    pallas_call x1, Pallas kernels, local_body(): pl.pallas_call(functools.partial(kernel, rows, d_model, q_heads, kv_heads...  27.6 us
    pallas_call x1, Pallas kernels, local_body(): pl.pallas_call(write_out, out_shape=(out, out), in_specs=[pl.BlockSpec(me...  1.16 us

profile of v2, /device:TPU:0, one launch (start us, length us, event | category | flops | bytes accessed | tf_op | source)
XLA Modules:
  0.0 29.6 jit_solution(629404929199009390)
XLA Ops:
  0.6 27.6 %shard_map.77 = (bf16[256,1536]{1,0:T(8,128)(2,1)S(1)}, bf16[256,1536]{1,0:T(8,128)(2,1)S(1)}) custom-call(bf16[256,1536]{1,0:T(8,128)(2,1)} %x_hbm.1, bf16[256,1536]{1,0:T(8,128)(2,1)} %dy_hbm.1, bf16[1536,1536]{1,0:T(8,128)(2,1)} %wq_hbm.1, bf16[1536,256]{1,0:T(8,128)(2,1)} %wk_hbm.1, bf16[1536,256]{1,0:T(8,128)(2,1)} %wv_hbm.1, bf16[1536,1536]{1,0:T(8,128)(2,1)} %wo_hbm.1), custom_call_target="tpu_custom_call" | custom-call | tf_op jit(solution)/shard_map/pallas_call | solution.py:327
  28.3 1.2 %shard_map.78 = (bf16[256,1536]{1,0:T(8,128)(2,1)}, bf16[256,1536]{1,0:T(8,128)(2,1)}) custom-call(bf16[256,1536]{1,0:T(8,128)(2,1)S(1)} %get-tuple-element.4.y_v, bf16[256,1536]{1,0:T(8,128)(2,1)S(1)} %get-tuple-element.5.dx_v), custom_call_target="tpu_custom_call" | custom-call | tf_op jit(solution)/shard_map/pallas_call | solution.py:368

commit v3 on v2

--- a/solution.py
+++ b/solution.py
@@ -10,6 +10,7 @@
 
 HEAD_DIM = 128
 CHUNK = 128
+SPLIT = 128
 MESH = pl.DeviceIdType.MESH
 F32 = jnp.float32
 BF16 = jnp.bfloat16
@@ -25,7 +26,7 @@
            x_hbm, dy_hbm, wq_hbm, wk_hbm, wv_hbm, wo_hbm,
            y_v, dx_v,
            x_v, dy_v, wq_v, wk_v, wv_v, wo_v,
-           qs, dot_v, k_all, v_all, kt, vt, pt, ds_t, e_buf, m_buf, l_buf, o_v, dq_v,
+           qs, dot_v, k_all, v_all, kt, vt, pt, ds_t, e_buf, m_buf, l_buf, f_buf, o_v, dq_v,
            part, recv_a, recv_b, recv_c, send_c, dx_acc,
            in_sem, ag_send, ag_recv, rs_send, rs_recv):
     group = q_heads // kv_heads
@@ -110,20 +111,23 @@
             m_buf[j, s * per_slot + c] = m8
             l_buf[j, s * per_slot + c] = jnp.sum(e, axis=0)
 
-    def finalize(i):
+    def finalize(i, slots):
         h, cols, _ = head_of(i)
         j = i % group
         n_chunks = 4 * per_slot
-        top = jnp.max(jnp.max(m_buf[j], axis=0), axis=0, keepdims=True)
-        factor = [jnp.exp2(m_buf[j, c] - top) for c in range(n_chunks)]
-        total = factor[0] * l_buf[j, 0]
-        for c in range(1, n_chunks):
-            total = total + factor[c] * l_buf[j, c]
-        inv = 1.0 / jnp.sum(total, axis=0, keepdims=True)
-        for c in range(n_chunks):
-            f8 = factor[c] * inv
-            e = e_buf[j, c * CHUNK:(c + 1) * CHUNK, :].reshape(CHUNK // 8, 8, rows)
-            pt[h, c * CHUNK:(c + 1) * CHUNK, cols] = (e * f8[None]).reshape(CHUNK, rows).astype(BF16)
+        if 3 in slots:
+            top = jnp.max(jnp.max(m_buf[j], axis=0), axis=0, keepdims=True)
+            factor = [jnp.exp2(m_buf[j, c] - top) for c in range(n_chunks)]
+            total = factor[0] * l_buf[j, 0]
+            for c in range(1, n_chunks):
+                total = total + factor[c] * l_buf[j, c]
+            inv = 1.0 / jnp.sum(total, axis=0, keepdims=True)
+            for c in range(n_chunks):
+                f_buf[j, c] = factor[c] * inv
+        for s in slots:
+            for c in range(s * per_slot, (s + 1) * per_slot):
+                e = e_buf[j, c * CHUNK:(c + 1) * CHUNK, :].reshape(CHUNK // 8, 8, rows)
+                pt[h, c * CHUNK:(c + 1) * CHUNK, cols] = (e * f_buf[j, c][None]).reshape(CHUNK, rows).astype(BF16)
 
     def outs(i):
         h, cols, feats = head_of(i)
@@ -142,13 +146,14 @@
 
     def grads(r, lo, hi):
         h = r % kv_heads
-        block = slice(lo * rows, hi * rows)
-        if r < kv_heads:
-            out = mm(pt[h, block, :], dot_v[h], NT)
-        else:
-            out = mm(ds_t[h, block, :], qs[h])
         for s in range(lo, hi):
-            part[r, s] = out[(s - lo) * rows:(s - lo + 1) * rows]
+            for t in range(rows // SPLIT):
+                block = slice(s * rows + t * SPLIT, s * rows + (t + 1) * SPLIT)
+                if r < kv_heads:
+                    out = mm(pt[h, block, :], dot_v[h], NT)
+                else:
+                    out = mm(ds_t[h, block, :], qs[h])
+                part[r, s, t * SPLIT:(t + 1) * SPLIT, :] = out
 
     def rs_copy(r, kind):
         src, dst, peer = ((part.at[r, 3], recv_a.at[r], partner),
@@ -166,109 +171,173 @@
 
     first = range(group)
     second = range(group, q_heads)
-
-    loads[0].wait()
-    loads[1].wait()
-    for w, copy, kv_ref in ((wk_v, None, k_all), (wv_v, loads[2], v_all)):
-        if copy is not None:
-            copy.wait()
+    n_pairs = q_heads // 4
+
+    peers = [partner, cross]
+
+    def stage(f):
+        peers.reverse()
+        pl.when(peers[0] != me)(f)
+
+    def project_kv(w, kv_ref):
         out = mm(x_v[...], w[...]).astype(BF16)
         for h in range(kv_heads):
             kv_ref[h, :rows, :] = out[:, h * d:(h + 1) * d]
-        if copy is None:
-            pl.semaphore_wait(barrier, 2)
+
+    def send_kv(item_of_head):
         for h in range(kv_heads):
-            i = 2 * h + (0 if copy is None else 1)
+            i = 2 * h + item_of_head
             ag_copy(i, 1).start()
             ag_copy(i, 0).start()
 
-    loads[3].wait()
-    for n in range(q_heads // 4):
-        project_q(n)
-    loads[4].wait()
-    ag_copy(0, 0).wait_recv()
-    for n in range(q_heads // 4):
-        project_q(q_heads // 4 + n)
-        for s in (0, 1):
-            scores(n, s)
-    loads[5].wait()
-    loads[6].wait()
-    for n in range(q_heads // 4):
-        project_do(n)
-        for s in (0, 1):
-            scores(q_heads // 4 + n, s)
-    loads[7].wait()
-    forward(0)
-    for n in range(q_heads // 4):
-        project_do(q_heads // 4 + n)
-        scores(2 * n, 2)
-        scores(2 * n + 1, 2)
-    ag_copy(0, 2).wait_recv()
-    for i in first:
-        scores(i, 3)
-    for i in first:
-        finalize(i)
-    forward(1)
-    grads(0, 3, 4)
-    rs_copy(0, 0).start()
-    grads(0, 2, 3)
-    ag_copy(2, 0).wait_recv()
-    for n in range(group):
-        scores(group + n, 0)
-        scores(group + n, 1)
-        if n == 0:
-            grads(0, 1, 2)
-        if n == 2:
-            grads(0, 0, 1)
-    forward(2)
-    reduce_cross(0)
-    rs_copy(0, 1).start()
-    ag_copy(1, 0).wait_recv()
-    ag_copy(1, 2).wait_recv()
-    transpose_item(1, vt)
-    for i in first:
-        outs(i)
-        scores(group + i, 2)
-    forward(3)
-    ag_copy(2, 2).wait_recv()
-    grads(2, 3, 4)
-    for i in second:
-        scores(i, 3)
-    rs_copy(2, 0).start()
-    grads(2, 2, 3)
-    for i in second:
-        finalize(i)
-    grads(1, 3, 4)
-    rs_copy(1, 0).start()
-    grads(1, 2, 3)
-    ag_copy(3, 0).wait_recv()
-    ag_copy(3, 2).wait_recv()
-    reduce_cross(2)
-    transpose_item(3, vt)
-    for i in range(group, group + group // 2):
-        outs(i)
-    reduce_cross(1)
-    for i in range(group + group // 2, q_heads):
-        outs(i)
-    grads(3, 3, 4)
-    rs_copy(3, 0).start()
-    grads(3, 2, 3)
-    for r in (2, 1):
-        grads(r, 0, 2)
-        rs_copy(r, 1).start()
-    reduce_cross(3)
-    grads(3, 0, 2)
-    rs_copy(3, 1).start()
-    transpose_item(0, kt)
-    transpose_item(2, kt)
-    for i in range(q_heads):
-        dqs(i)
-    for n in range(d_model // 256):
-        cols = slice(n * 256, (n + 1) * 256)
-        y_v[:, cols] = mm(o_v[...], wo_v[:, cols]).astype(BF16)
-    for n in range(d_model // 256):
-        cols = slice(n * 256, (n + 1) * 256)
-        dx_acc[:, cols] = mm(dq_v[...], wq_v[cols, :], NT)
+    @stage
+    def _():
+        loads[0].wait()
+        loads[1].wait()
+        project_kv(wk_v, k_all)
+
+    pl.semaphore_wait(barrier, 2)
+    send_kv(0)
+
+    @stage
+    def _():
+        loads[2].wait()
+        project_kv(wv_v, v_all)
+
+    send_kv(1)
+
+    @stage
+    def _():
+        loads[3].wait()
+        for n in range(n_pairs):
+            project_q(n)
+
+    @stage
+    def _():
+        loads[4].wait()
+        ag_copy(0, 0).wait_recv()
+        for n in range(n_pairs):
+            project_q(n_pairs + n)
+            for i in (2 * n, 2 * n + 1):
+                scores(i, 0)
+                scores(i, 1)
+
+    @stage
+    def _():
+        loads[5].wait()
+        loads[6].wait()
+        for n in range(n_pairs):
+            project_do(n)
+
+    @stage
+    def _():
+        loads[7].wait()
+        forward(0)
+        for n in range(n_pairs):
+            project_do(n_pairs + n)
+            scores(2 * n, 2)
+            scores(2 * n + 1, 2)
+
+    @stage
+    def _():
+        ag_copy(0, 2).wait_recv()
+        for i in first:
+            scores(i, 3)
+        for i in first:
+            finalize(i, (3, 2))
+
+    @stage
+    def _():
+        forward(1)
+        grads(0, 3, 4)
+        rs_copy(0, 0).start()
+        grads(0, 2, 3)
+        for n in first:
+            finalize(n, (1, 0))
+
+    @stage
+    def _():
+        ag_copy(2, 0).wait_recv()
+        for n in range(group):
+            scores(group + n, 0)
+            if n == 0:
+                grads(0, 1, 2)
+            if n == 3:
+                grads(0, 0, 1)
+            scores(group + n, 1)
+        rs_copy(0, 1).start()
+
+    @stage
+    def _():
+        forward(2)
+        reduce_cross(0)
+        ag_copy(1, 0).wait_recv()
+        ag_copy(1, 2).wait_recv()
+        transpose_item(1, vt)
+        for i in first:
+            outs(i)
+            scores(group + i, 2)
+
+    @stage
+    def _():
+        forward(3)
+        ag_copy(2, 2).wait_recv()
+        grads(2, 3, 4)
+        rs_copy(2, 0).start()
+        for i in second:
+            scores(i, 3)
+        for i in second:
+            finalize(i, (3, 2))
+        grads(2, 2, 3)
+
+    @stage
+    def _():
+        grads(1, 3, 4)
+        rs_copy(1, 0).start()
+        grads(1, 2, 3)
+        for i in second:
+            finalize(i, (1, 0))
+
+    @stage
+    def _():
+        reduce_cross(2)
+        ag_copy(3, 0).wait_recv()
+        ag_copy(3, 2).wait_recv()
+        transpose_item(3, vt)
+        for i in second[:group // 2]:
+            outs(i)
+
+    @stage
+    def _():
+        reduce_cross(1)
+        for i in second[group // 2:]:
+            outs(i)
+
+    @stage
+    def _():
+        grads(3, 3, 4)
+        rs_copy(3, 0).start()
+        grads(3, 2, 3)
+        grads(2, 0, 2)
+        rs_copy(2, 1).start()
+        grads(1, 0, 2)
+        rs_copy(1, 1).start()
+
+    @stage
+    def _():
+        reduce_cross(3)
+        grads(3, 0, 2)
+        rs_copy(3, 1).start()
+        transpose_item(0, kt)
+        transpose_item(2, kt)
+        for i in range(q_heads):
+            dqs(i)
+        for n in range(d_model // 256):
+            cols = slice(n * 256, (n + 1) * 256)
+            y_v[:, cols] = mm(o_v[...], wo_v[:, cols]).astype(BF16)
+        for n in range(d_model // 256):
+            cols = slice(n * 256, (n + 1) * 256)
+            dx_acc[:, cols] = mm(dq_v[...], wq_v[cols, :], NT)
 
     def own(r):
         rs_copy(r, 1).wait_recv()
@@ -278,25 +347,33 @@
             total = total * scale
         return total.astype(BF16)
 
-    for r in (0, 2, 1):
-        g = own(r)
+    def add_own(r, g):
         h = r % kv_heads
         w = wv_v if r < kv_heads else wk_v
         for n in range(d_model // 256):
             cols = slice(n * 256, (n + 1) * 256)
-            dx_acc[:, cols] += mm(g, w[cols, h * d:(h + 1) * d], NT)
-    g = own(3)
-    for n in range(d_model // 256):
-        cols = slice(n * 256, (n + 1) * 256)
-        total = dx_acc[:, cols] + mm(g, wk_v[cols, d:2 * d], NT)
-        dx_v[:, cols] = total.astype(BF16)
+            yield cols, dx_acc[:, cols] + mm(g, w[cols, h * d:(h + 1) * d], NT)
+
+    for r in (0, 2, 1):
+        @stage
+        def _(r=r):
+            for cols, total in add_own(r, own(r)):
+                dx_acc[:, cols] = total
 
     for i in range(2 * kv_heads):
         for hop in range(3):
             ag_copy(i, hop).wait_send()
     for r in range(2 * kv_heads):
         for kind in range(3):
-            rs_copy(r, kind).wait_send()
+            if (r, kind) != (3, 2):
+                rs_copy(r, kind).wait_send()
+
+    @stage
+    def _():
+        for cols, total in add_own(3, own(3)):
+            dx_v[:, cols] = total.astype(BF16)
+
+    rs_copy(3, 2).wait_send()
 
 
 def write_out(y_v, dx_v, y_hbm, dx_hbm, sem):
@@ -347,6 +424,7 @@
                 pltpu.VMEM((group, n_keys, rows), F32),
                 pltpu.VMEM((group, n_keys // CHUNK, 8, rows), F32),
                 pltpu.VMEM((group, n_keys // CHUNK, 8, rows), F32),
+                pltpu.VMEM((group, n_keys // CHUNK, 8, rows), F32),
                 pltpu.VMEM((rows, qw), BF16),
                 pltpu.VMEM((rows, qw), BF16),
                 pltpu.VMEM((items, 4, rows, d), F32),

time: 29.7 us -> 29.5 us (level)
  no operation moved by 1% of the time
where the time goes in v3:
time: 29.5 us; the launch traced here: 29.4 us
  Pallas kernels  28.6 us (97%)
  between operations  0.8 us (3%)
    pallas_call x1, Pallas kernels, local_body(): pl.pallas_call(functools.partial(kernel, rows, d_model, q_heads, kv_heads...  27.5 us
    pallas_call x1, Pallas kernels, local_body(): pl.pallas_call(write_out, out_shape=(out, out), in_specs=[pl.BlockSpec(me...  1.16 us

profile of v3, /device:TPU:0, one launch (start us, length us, event | category | flops | bytes accessed | tf_op | source)
XLA Modules:
  0.0 29.4 jit_solution(10053651000678861730)
XLA Ops:
  0.6 27.5 %shard_map.77 = (bf16[256,1536]{1,0:T(8,128)(2,1)S(1)}, bf16[256,1536]{1,0:T(8,128)(2,1)S(1)}) custom-call(bf16[256,1536]{1,0:T(8,128)(2,1)} %x_hbm.1, bf16[256,1536]{1,0:T(8,128)(2,1)} %dy_hbm.1, bf16[1536,1536]{1,0:T(8,128)(2,1)} %wq_hbm.1, bf16[1536,256]{1,0:T(8,128)(2,1)} %wk_hbm.1, bf16[1536,256]{1,0:T(8,128)(2,1)} %wv_hbm.1, bf16[1536,1536]{1,0:T(8,128)(2,1)} %wo_hbm.1), custom_call_target="tpu_custom_call" | custom-call | tf_op jit(solution)/shard_map/pallas_call | solution.py:404
  28.1 1.2 %shard_map.78 = (bf16[256,1536]{1,0:T(8,128)(2,1)}, bf16[256,1536]{1,0:T(8,128)(2,1)}) custom-call(bf16[256,1536]{1,0:T(8,128)(2,1)S(1)} %get-tuple-element.4.y_v, bf16[256,1536]{1,0:T(8,128)(2,1)S(1)} %get-tuple-element.5.dx_v), custom_call_target="tpu_custom_call" | custom-call | tf_op jit(solution)/shard_map/pallas_call | solution.py:446

commit v4 on v3

--- a/solution.py
+++ b/solution.py
@@ -69,7 +69,7 @@
         src, dst, peer = ((0, 1, partner), (0, 2, cross), (2, 3, partner))[hop]
         return pltpu.make_async_remote_copy(
             src_ref=slot(i, src), dst_ref=slot(i, dst),
-            send_sem=ag_send.at[i, hop], recv_sem=ag_recv.at[i, hop],
+            send_sem=ag_send, recv_sem=ag_recv.at[i, hop],
             device_id={"cp": peer}, device_id_type=MESH)
 
     def forward(i):
@@ -100,7 +100,7 @@
 
     def scores(i, s):
         h, cols, _ = head_of(i)
-        j = i % group
+        j = i
         raw = mm(k_all[h, s * rows:(s + 1) * rows, :], qs[h, cols, :], NT)
         for c in range(per_slot):
             t = raw[c * CHUNK:(c + 1) * CHUNK] * gain
@@ -113,7 +113,7 @@
 
     def finalize(i, slots):
         h, cols, _ = head_of(i)
-        j = i % group
+        j = i
         n_chunks = 4 * per_slot
         if 3 in slots:
             top = jnp.max(jnp.max(m_buf[j], axis=0), axis=0, keepdims=True)
@@ -129,16 +129,27 @@
                 e = e_buf[j, c * CHUNK:(c + 1) * CHUNK, :].reshape(CHUNK // 8, 8, rows)
                 pt[h, c * CHUNK:(c + 1) * CHUNK, cols] = (e * f_buf[j, c][None]).reshape(CHUNK, rows).astype(BF16)
 
-    def outs(i):
+    def out_head(i):
         h, cols, feats = head_of(i)
         o_t = mm(vt[h], pt[h, :, cols]).astype(BF16)
         o_v[:, feats] = o_t.T
+        return jnp.sum(dot_v[h, :, cols].astype(F32) * o_t.astype(F32), axis=0, keepdims=True)
+
+    def dscore(i, delta):
+        h, cols, _ = head_of(i)
         do_t = dot_v[h, :, cols]
-        delta = jnp.sum(do_t.astype(F32) * o_t.astype(F32), axis=0, keepdims=True)
         for s in range(4):
             keys = slice(s * rows, (s + 1) * rows)
             dp = mm(v_all[h, keys, :], do_t)
             ds_t[h, keys, cols] = (pt[h, keys, cols].astype(F32) * (dp - delta)).astype(BF16)
+
+    def out_all(heads):
+        heads = list(heads)
+        delta = out_head(heads[0])
+        for i, after in zip(heads, heads[1:] + [None]):
+            delta_after = None if after is None else out_head(after)
+            dscore(i, delta)
+            delta = delta_after
 
     def dqs(i):
         h, cols, feats = head_of(i)
@@ -161,7 +172,7 @@
                           (send_c.at[r], recv_c.at[r], cross))[kind]
         return pltpu.make_async_remote_copy(
             src_ref=src, dst_ref=dst,
-            send_sem=rs_send.at[r, kind], recv_sem=rs_recv.at[r, kind],
+            send_sem=rs_send, recv_sem=rs_recv.at[r, kind],
             device_id={"cp": peer}, device_id_type=MESH)
 
     def reduce_cross(r):
@@ -226,154 +237,151 @@
     def _():
         loads[5].wait()
         loads[6].wait()
+        ag_copy(2, 0).wait_recv()
         for n in range(n_pairs):
             project_do(n)
+            for i in (2 * n, 2 * n + 1):
+                scores(group + i, 0)
+                scores(group + i, 1)
 
     @stage
     def _():
         loads[7].wait()
         forward(0)
         for n in range(n_pairs):
-            project_do(n_pairs + n)
+            if n == 0:
+                project_do(n_pairs)
             scores(2 * n, 2)
             scores(2 * n + 1, 2)
 
     @stage
     def _():
         ag_copy(0, 2).wait_recv()
-        for i in first:
-            scores(i, 3)
-        for i in first:
-            finalize(i, (3, 2))
+        for n in range(n_pairs):
+            scores(2 * n, 3)
+            scores(2 * n + 1, 3)
+            if n > 0:
+                project_do(n_pairs + n)
+            finalize(2 * n, (3, 2))
+            finalize(2 * n + 1, (3, 2))
 
     @stage
     def _():
         forward(1)
         grads(0, 3, 4)
-        rs_copy(0, 0).start()
         grads(0, 2, 3)
         for n in first:
             finalize(n, (1, 0))
-
-    @stage
-    def _():
-        ag_copy(2, 0).wait_recv()
+        rs_copy(0, 0).start()
+
+    @stage
+    def _():
+        forward(2)
         for n in range(group):
-            scores(group + n, 0)
-            if n == 0:
+            scores(group + n, 2)
+            if n == 1:
                 grads(0, 1, 2)
             if n == 3:
                 grads(0, 0, 1)
-            scores(group + n, 1)
         rs_copy(0, 1).start()
 
     @stage
     def _():
-        forward(2)
         reduce_cross(0)
         ag_copy(1, 0).wait_recv()
         ag_copy(1, 2).wait_recv()
         transpose_item(1, vt)
-        for i in first:
-            outs(i)
-            scores(group + i, 2)
+        out_all(first)
 
     @stage
     def _():
         forward(3)
         ag_copy(2, 2).wait_recv()
-        grads(2, 3, 4)
+        for n in range(n_pairs):
+            scores(group + 2 * n, 3)
+            scores(group + 2 * n + 1, 3)
+            if n > 0:
+                grads(2, 4 - n, 5 - n)
+            finalize(group + 2 * n, (3, 2))
+            finalize(group + 2 * n + 1, (3, 2))
         rs_copy(2, 0).start()
-        for i in second:
-            scores(i, 3)
-        for i in second:
-            finalize(i, (3, 2))
-        grads(2, 2, 3)
 
     @stage
     def _():
         grads(1, 3, 4)
-        rs_copy(1, 0).start()
         grads(1, 2, 3)
         for i in second:
             finalize(i, (1, 0))
-
-    @stage
-    def _():
-        reduce_cross(2)
+        rs_copy(1, 0).start()
+
+    @stage
+    def _():
         ag_copy(3, 0).wait_recv()
         ag_copy(3, 2).wait_recv()
         transpose_item(3, vt)
-        for i in second[:group // 2]:
-            outs(i)
-
-    @stage
-    def _():
-        reduce_cross(1)
-        for i in second[group // 2:]:
-            outs(i)
-
-    @stage
-    def _():
-        grads(3, 3, 4)
-        rs_copy(3, 0).start()
-        grads(3, 2, 3)
+        out_all(second[:group // 2])
         grads(2, 0, 2)
         rs_copy(2, 1).start()
+
+    @stage
+    def _():
+        reduce_cross(2)
+        out_all(second[group // 2:])
+
+    @stage
+    def _():
+        reduce_cross(1)
+        grads(3, 3, 4)
+        grads(3, 2, 3)
         grads(1, 0, 2)
+        rs_copy(3, 0).start()
         rs_copy(1, 1).start()
 
     @stage
     def _():
+        grads(3, 0, 2)
+        transpose_item(0, kt)
+        for i in first:
+            dqs(i)
+        transpose_item(2, kt)
+        for i in second:
+            dqs(i)
+        rs_copy(3, 1).start()
+
+    @stage
+    def _():
         reduce_cross(3)
-        grads(3, 0, 2)
-        rs_copy(3, 1).start()
-        transpose_item(0, kt)
-        transpose_item(2, kt)
-        for i in range(q_heads):
-            dqs(i)
         for n in range(d_model // 256):
             cols = slice(n * 256, (n + 1) * 256)
             y_v[:, cols] = mm(o_v[...], wo_v[:, cols]).astype(BF16)
+
+    def own(items, factor):
+        parts = []
+        for r in items:
+            rs_copy(r, 1).wait_recv()
+            rs_copy(r, 2).wait_recv()
+        for r in items:
+            total = part[r, 0] + recv_b[r] + recv_c[r]
+            parts.append((total * factor).astype(BF16) if factor != 1 else total.astype(BF16))
+        return jnp.concatenate(parts, axis=1)
+
+    @stage
+    def _():
+        dv = own((0, 1), 1)
         for n in range(d_model // 256):
             cols = slice(n * 256, (n + 1) * 256)
-            dx_acc[:, cols] = mm(dq_v[...], wq_v[cols, :], NT)
-
-    def own(r):
-        rs_copy(r, 1).wait_recv()
-        rs_copy(r, 2).wait_recv()
-        total = part[r, 0] + recv_b[r] + recv_c[r]
-        if r >= kv_heads:
-            total = total * scale
-        return total.astype(BF16)
-
-    def add_own(r, g):
-        h = r % kv_heads
-        w = wv_v if r < kv_heads else wk_v
+            dx_acc[:, cols] = mm(dq_v[...], wq_v[cols, :], NT) + mm(dv, wv_v[cols, :], NT)
+
+    pltpu.make_async_copy(x_v, x_v, ag_send).wait()
+
+    @stage
+    def _():
+        dk = own((2, 3), scale)
         for n in range(d_model // 256):
             cols = slice(n * 256, (n + 1) * 256)
-            yield cols, dx_acc[:, cols] + mm(g, w[cols, h * d:(h + 1) * d], NT)
-
-    for r in (0, 2, 1):
-        @stage
-        def _(r=r):
-            for cols, total in add_own(r, own(r)):
-                dx_acc[:, cols] = total
-
-    for i in range(2 * kv_heads):
-        for hop in range(3):
-            ag_copy(i, hop).wait_send()
-    for r in range(2 * kv_heads):
-        for kind in range(3):
-            if (r, kind) != (3, 2):
-                rs_copy(r, kind).wait_send()
-
-    @stage
-    def _():
-        for cols, total in add_own(3, own(3)):
-            dx_v[:, cols] = total.astype(BF16)
-
-    rs_copy(3, 2).wait_send()
+            dx_v[:, cols] = (dx_acc[:, cols] + mm(dk, wk_v[cols, :], NT)).astype(BF16)
+
+    pltpu.make_async_copy(dx_acc, dx_acc, rs_send).wait()
 
 
 def write_out(y_v, dx_v, y_hbm, dx_hbm, sem):
@@ -421,10 +429,10 @@
                 pltpu.VMEM((kv_heads, d, n_keys), BF16),
                 pltpu.VMEM((kv_heads, n_keys, group * rows), BF16),
                 pltpu.VMEM((kv_heads, n_keys, group * rows), BF16),
-                pltpu.VMEM((group, n_keys, rows), F32),
-                pltpu.VMEM((group, n_keys // CHUNK, 8, rows), F32),
-                pltpu.VMEM((group, n_keys // CHUNK, 8, rows), F32),
-                pltpu.VMEM((group, n_keys // CHUNK, 8, rows), F32),
+                pltpu.VMEM((q_heads, n_keys, rows), F32),
+                pltpu.VMEM((q_heads, n_keys // CHUNK, 8, rows), F32),
+                pltpu.VMEM((q_heads, n_keys // CHUNK, 8, rows), F32),
+                pltpu.VMEM((q_heads, n_keys // CHUNK, 8, rows), F32),
                 pltpu.VMEM((rows, qw), BF16),
                 pltpu.VMEM((rows, qw), BF16),
                 pltpu.VMEM((items, 4, rows, d), F32),
@@ -434,14 +442,14 @@
                 pltpu.VMEM((items, rows, d), F32),
                 pltpu.VMEM((rows, d_model), F32),
                 pltpu.SemaphoreType.DMA((8,)),
+                pltpu.SemaphoreType.DMA,
                 pltpu.SemaphoreType.DMA((items, 3)),
-                pltpu.SemaphoreType.DMA((items, 3)),
-                pltpu.SemaphoreType.DMA((items, 3)),
+                pltpu.SemaphoreType.DMA,
                 pltpu.SemaphoreType.DMA((items, 3)),
             ],
             compiler_params=pltpu.CompilerParams(
                 collective_id=0, has_side_effects=True,
-                vmem_limit_bytes=50 * 1024 * 1024),
+                vmem_limit_bytes=52 * 1024 * 1024),
         )(*(pltpu.with_memory_space_constraint(a, pltpu.HBM) for a in (x_loc, dy_loc, w_q, w_k, w_v, w_o)))
         return pl.pallas_call(
             write_out,

time: 29.5 us -> 29.9 us (1.014)
  Pallas kernels: 28.6 us -> 29 us
    pallas_call x1, Pallas kernels: 27.5 us -> 27.8 us  [local_body(): pl.pallas_call(functools.partial(kernel, rows, d_model, q_heads, kv_heads...]
where the time goes in v4:
time: 29.9 us; the launch traced here: 29.8 us
  Pallas kernels  29 us (97%)
  between operations  0.8 us (3%)
    pallas_call x1, Pallas kernels, local_body(): pl.pallas_call(functools.partial(kernel, rows, d_model, q_heads, kv_heads...  27.8 us
    pallas_call x1, Pallas kernels, local_body(): pl.pallas_call(write_out, out_shape=(out, out), in_specs=[pl.BlockSpec(me...  1.16 us

profile of v4, /device:TPU:0, one launch (start us, length us, event | category | flops | bytes accessed | tf_op | source)
XLA Modules:
  0.0 29.8 jit_solution(15484921420646039061)
XLA Ops:
  0.6 27.8 %shard_map.77 = (bf16[256,1536]{1,0:T(8,128)(2,1)S(1)}, bf16[256,1536]{1,0:T(8,128)(2,1)S(1)}) custom-call(bf16[256,1536]{1,0:T(8,128)(2,1)} %x_hbm.1, bf16[256,1536]{1,0:T(8,128)(2,1)} %dy_hbm.1, bf16[1536,1536]{1,0:T(8,128)(2,1)} %wq_hbm.1, bf16[1536,256]{1,0:T(8,128)(2,1)} %wk_hbm.1, bf16[1536,256]{1,0:T(8,128)(2,1)} %wv_hbm.1, bf16[1536,1536]{1,0:T(8,128)(2,1)} %wo_hbm.1), custom_call_target="tpu_custom_call" | custom-call | tf_op jit(solution)/shard_map/pallas_call | solution.py:412
  28.5 1.2 %shard_map.78 = (bf16[256,1536]{1,0:T(8,128)(2,1)}, bf16[256,1536]{1,0:T(8,128)(2,1)}) custom-call(bf16[256,1536]{1,0:T(8,128)(2,1)S(1)} %get-tuple-element.4.y_v, bf16[256,1536]{1,0:T(8,128)(2,1)S(1)} %get-tuple-element.5.dx_v), custom_call_target="tpu_custom_call" | custom-call | tf_op jit(solution)/shard_map/pallas_call | solution.py:454

commit v5 on v4

--- a/solution.py
+++ b/solution.py
@@ -240,17 +240,23 @@
         ag_copy(2, 0).wait_recv()
         for n in range(n_pairs):
             project_do(n)
-            for i in (2 * n, 2 * n + 1):
-                scores(group + i, 0)
-                scores(group + i, 1)
+            scores(group + n, 0)
+            scores(group + n, 1)
 
     @stage
     def _():
         loads[7].wait()
         forward(0)
-        for n in range(n_pairs):
-            if n == 0:
-                project_do(n_pairs)
+        project_do(n_pairs)
+        for n in range(n_pairs):
+            scores(group + n_pairs + n, 0)
+            scores(group + n_pairs + n, 1)
+
+    @stage
+    def _():
+        for n in range(n_pairs):
+            if n > 0:
+                project_do(n_pairs + n)
             scores(2 * n, 2)
             scores(2 * n + 1, 2)
 
@@ -260,8 +266,6 @@
         for n in range(n_pairs):
             scores(2 * n, 3)
             scores(2 * n + 1, 3)
-            if n > 0:
-                project_do(n_pairs + n)
             finalize(2 * n, (3, 2))
             finalize(2 * n + 1, (3, 2))
 
@@ -269,10 +273,13 @@
     def _():
         forward(1)
         grads(0, 3, 4)
+        rs_copy(0, 0).start()
+
+    @stage
+    def _():
         grads(0, 2, 3)
         for n in first:
             finalize(n, (1, 0))
-        rs_copy(0, 0).start()
 
     @stage
     def _():
@@ -281,47 +288,56 @@
             scores(group + n, 2)
             if n == 1:
                 grads(0, 1, 2)
-            if n == 3:
+
+    @stage
+    def _():
+        reduce_cross(0)
+        rs_copy(0, 1).start()
+        ag_copy(2, 2).wait_recv()
+        for n in range(n_pairs):
+            scores(group + 2 * n, 3)
+            scores(group + 2 * n + 1, 3)
+            if n == 1:
                 grads(0, 0, 1)
-        rs_copy(0, 1).start()
-
-    @stage
-    def _():
-        reduce_cross(0)
+            finalize(group + 2 * n, (3, 2))
+            finalize(group + 2 * n + 1, (3, 2))
+
+    @stage
+    def _():
+        forward(3)
+        grads(1, 3, 4)
+        rs_copy(1, 0).start()
+
+    @stage
+    def _():
         ag_copy(1, 0).wait_recv()
         ag_copy(1, 2).wait_recv()
         transpose_item(1, vt)
-        out_all(first)
-
-    @stage
-    def _():
-        forward(3)
-        ag_copy(2, 2).wait_recv()
-        for n in range(n_pairs):
-            scores(group + 2 * n, 3)
-            scores(group + 2 * n + 1, 3)
-            if n > 0:
-                grads(2, 4 - n, 5 - n)
-            finalize(group + 2 * n, (3, 2))
-            finalize(group + 2 * n + 1, (3, 2))
-        rs_copy(2, 0).start()
-
-    @stage
-    def _():
-        grads(1, 3, 4)
         grads(1, 2, 3)
         for i in second:
             finalize(i, (1, 0))
-        rs_copy(1, 0).start()
+
+    @stage
+    def _():
+        out_all(first[:group // 2])
+
+    @stage
+    def _():
+        reduce_cross(1)
+        out_all(first[group // 2:])
+
+    @stage
+    def _():
+        grads(2, 3, 4)
+        rs_copy(2, 0).start()
 
     @stage
     def _():
         ag_copy(3, 0).wait_recv()
         ag_copy(3, 2).wait_recv()
         transpose_item(3, vt)
+        grads(2, 2, 3)
         out_all(second[:group // 2])
-        grads(2, 0, 2)
-        rs_copy(2, 1).start()
 
     @stage
     def _():
@@ -330,27 +346,28 @@
 
     @stage
     def _():
-        reduce_cross(1)
         grads(3, 3, 4)
+        rs_copy(3, 0).start()
+
+    @stage
+    def _():
         grads(3, 2, 3)
         grads(1, 0, 2)
-        rs_copy(3, 0).start()
+        grads(2, 0, 2)
+        grads(3, 0, 2)
         rs_copy(1, 1).start()
-
-    @stage
-    def _():
-        grads(3, 0, 2)
+        rs_copy(2, 1).start()
+        rs_copy(3, 1).start()
+
+    @stage
+    def _():
+        reduce_cross(3)
         transpose_item(0, kt)
         for i in first:
             dqs(i)
         transpose_item(2, kt)
         for i in second:
             dqs(i)
-        rs_copy(3, 1).start()
-
-    @stage
-    def _():
-        reduce_cross(3)
         for n in range(d_model // 256):
             cols = slice(n * 256, (n + 1) * 256)
             y_v[:, cols] = mm(o_v[...], wo_v[:, cols]).astype(BF16)

time: 29.9 us -> 28 us (0.936)
  Pallas kernels: 29 us -> 27.1 us
    pallas_call x1, Pallas kernels: 27.8 us -> 26 us  [local_body(): pl.pallas_call(functools.partial(kernel, rows, d_model, q_heads, kv_heads...]
where the time goes in v5:
time: 28 us; the launch traced here: 27.9 us
  Pallas kernels  27.1 us (97%)
  between operations  0.8 us (3%)
    pallas_call x1, Pallas kernels, local_body(): pl.pallas_call(functools.partial(kernel, rows, d_model, q_heads, kv_heads...  26 us
    pallas_call x1, Pallas kernels, local_body(): pl.pallas_call(write_out, out_shape=(out, out), in_specs=[pl.BlockSpec(me...  1.16 us

profile of v5, /device:TPU:0, one launch (start us, length us, event | category | flops | bytes accessed | tf_op | source)
XLA Modules:
  0.0 27.9 jit_solution(6192730964679260356)
XLA Ops:
  0.6 26.0 %shard_map.77 = (bf16[256,1536]{1,0:T(8,128)(2,1)S(1)}, bf16[256,1536]{1,0:T(8,128)(2,1)S(1)}) custom-call(bf16[256,1536]{1,0:T(8,128)(2,1)} %x_hbm.1, bf16[256,1536]{1,0:T(8,128)(2,1)} %dy_hbm.1, bf16[1536,1536]{1,0:T(8,128)(2,1)} %wq_hbm.1, bf16[1536,256]{1,0:T(8,128)(2,1)} %wk_hbm.1, bf16[1536,256]{1,0:T(8,128)(2,1)} %wv_hbm.1, bf16[1536,1536]{1,0:T(8,128)(2,1)} %wo_hbm.1), custom_call_target="tpu_custom_call" | custom-call | tf_op jit(solution)/shard_map/pallas_call | solution.py:429
  26.6 1.2 %shard_map.78 = (bf16[256,1536]{1,0:T(8,128)(2,1)}, bf16[256,1536]{1,0:T(8,128)(2,1)}) custom-call(bf16[256,1536]{1,0:T(8,128)(2,1)S(1)} %get-tuple-element.4.y_v, bf16[256,1536]{1,0:T(8,128)(2,1)S(1)} %get-tuple-element.5.dx_v), custom_call_target="tpu_custom_call" | custom-call | tf_op jit(solution)/shard_map/pallas_call | solution.py:471

commit v6 on v5

--- a/solution.py
+++ b/solution.py
@@ -11,6 +11,7 @@
 HEAD_DIM = 128
 CHUNK = 128
 SPLIT = 128
+WRITES = 4
 MESH = pl.DeviceIdType.MESH
 F32 = jnp.float32
 BF16 = jnp.bfloat16
@@ -103,10 +104,9 @@
         j = i
         raw = mm(k_all[h, s * rows:(s + 1) * rows, :], qs[h, cols, :], NT)
         for c in range(per_slot):
-            t = raw[c * CHUNK:(c + 1) * CHUNK] * gain
-            t = t.reshape(CHUNK // 8, 8, rows)
-            m8 = jnp.max(t, axis=0)
-            e = jnp.exp2(t - m8[None])
+            t = raw[c * CHUNK:(c + 1) * CHUNK].reshape(CHUNK // 8, 8, rows)
+            m8 = jnp.max(t, axis=0) * gain
+            e = jnp.exp2(t * gain - m8[None])
             e_buf[j, s * rows + c * CHUNK:s * rows + (c + 1) * CHUNK, :] = e.reshape(CHUNK, rows)
             m_buf[j, s * per_slot + c] = m8
             l_buf[j, s * per_slot + c] = jnp.sum(e, axis=0)
@@ -245,90 +245,63 @@
 
     @stage
     def _():
-        loads[7].wait()
         forward(0)
-        project_do(n_pairs)
         for n in range(n_pairs):
             scores(group + n_pairs + n, 0)
             scores(group + n_pairs + n, 1)
-
-    @stage
-    def _():
+        for n in first:
+            scores(n, 2)
+
+    def normalize_far(heads, r):
+        for i in heads:
+            scores(i, 3)
+            if i > heads[0]:
+                finalize(i - 1, (3, 2))
+        finalize(heads[-1], (3, 2))
+        grads(r, 3, 4)
+        grads(r, 2, 3)
+        rs_copy(r, 0).start()
+
+    @stage
+    def _():
+        ag_copy(0, 2).wait_recv()
+        normalize_far(first, 0)
+
+    @stage
+    def _():
+        loads[7].wait()
+        forward(1)
+        forward(2)
         for n in range(n_pairs):
-            if n > 0:
-                project_do(n_pairs + n)
-            scores(2 * n, 2)
-            scores(2 * n + 1, 2)
-
-    @stage
-    def _():
-        ag_copy(0, 2).wait_recv()
-        for n in range(n_pairs):
-            scores(2 * n, 3)
-            scores(2 * n + 1, 3)
-            finalize(2 * n, (3, 2))
-            finalize(2 * n + 1, (3, 2))
-
-    @stage
-    def _():
-        forward(1)
-        grads(0, 3, 4)
-        rs_copy(0, 0).start()
-
-    @stage
-    def _():
-        grads(0, 2, 3)
-        for n in first:
-            finalize(n, (1, 0))
-
-    @stage
-    def _():
-        forward(2)
-        for n in range(group):
-            scores(group + n, 2)
-            if n == 1:
-                grads(0, 1, 2)
+            project_do(n_pairs + n)
+            for i in (2 * n, 2 * n + 1):
+                finalize(i, (1, 0))
+                scores(group + i, 2)
+        grads(0, 1, 2)
 
     @stage
     def _():
         reduce_cross(0)
         rs_copy(0, 1).start()
         ag_copy(2, 2).wait_recv()
-        for n in range(n_pairs):
-            scores(group + 2 * n, 3)
-            scores(group + 2 * n + 1, 3)
-            if n == 1:
-                grads(0, 0, 1)
-            finalize(group + 2 * n, (3, 2))
-            finalize(group + 2 * n + 1, (3, 2))
+        normalize_far(second, 1)
 
     @stage
     def _():
         forward(3)
-        grads(1, 3, 4)
-        rs_copy(1, 0).start()
-
-    @stage
-    def _():
         ag_copy(1, 0).wait_recv()
         ag_copy(1, 2).wait_recv()
         transpose_item(1, vt)
-        grads(1, 2, 3)
         for i in second:
             finalize(i, (1, 0))
-
-    @stage
-    def _():
         out_all(first[:group // 2])
 
     @stage
     def _():
         reduce_cross(1)
         out_all(first[group // 2:])
-
-    @stage
-    def _():
         grads(2, 3, 4)
+        grads(2, 2, 3)
         rs_copy(2, 0).start()
 
     @stage
@@ -336,38 +309,35 @@
         ag_copy(3, 0).wait_recv()
         ag_copy(3, 2).wait_recv()
         transpose_item(3, vt)
-        grads(2, 2, 3)
+        grads(0, 0, 1)
         out_all(second[:group // 2])
 
     @stage
     def _():
         reduce_cross(2)
         out_all(second[group // 2:])
-
-    @stage
-    def _():
         grads(3, 3, 4)
+        grads(3, 2, 3)
         rs_copy(3, 0).start()
 
     @stage
     def _():
-        grads(3, 2, 3)
         grads(1, 0, 2)
         grads(2, 0, 2)
-        grads(3, 0, 2)
         rs_copy(1, 1).start()
         rs_copy(2, 1).start()
-        rs_copy(3, 1).start()
 
     @stage
     def _():
         reduce_cross(3)
+        grads(3, 0, 2)
         transpose_item(0, kt)
         for i in first:
             dqs(i)
         transpose_item(2, kt)
         for i in second:
             dqs(i)
+        rs_copy(3, 1).start()
         for n in range(d_model // 256):
             cols = slice(n * 256, (n + 1) * 256)
             y_v[:, cols] = mm(o_v[...], wo_v[:, cols]).astype(BF16)
@@ -402,8 +372,12 @@
 
 
 def write_out(y_v, dx_v, y_hbm, dx_hbm, sem):
-    copies = [pltpu.make_async_copy(y_v, y_hbm, sem.at[0]),
-              pltpu.make_async_copy(dx_v, dx_hbm, sem.at[1])]
+    n = y_v.shape[0] // WRITES
+    copies = []
+    for i in range(WRITES):
+        part = slice(i * n, (i + 1) * n)
+        copies.append(pltpu.make_async_copy(dx_v.at[part], dx_hbm.at[part], sem.at[2 * i]))
+        copies.append(pltpu.make_async_copy(y_v.at[part], y_hbm.at[part], sem.at[2 * i + 1]))
     for copy in copies:
         copy.start()
     for copy in copies:
@@ -473,7 +447,7 @@
             out_shape=(out, out),
             in_specs=[pl.BlockSpec(memory_space=pl.ANY)] * 2,
             out_specs=(hbm, hbm),
-            scratch_shapes=[pltpu.SemaphoreType.DMA((2,))],
+            scratch_shapes=[pltpu.SemaphoreType.DMA((2 * WRITES,))],
             compiler_params=pltpu.CompilerParams(vmem_limit_bytes=4 * 1024 * 1024),
         )(y_v, dx_v)
 

time: 28 us -> 27.5 us (0.982)
  Pallas kernels: 27.1 us -> 26.6 us
    pallas_call x1, Pallas kernels: 26 us -> 25.4 us  [local_body(): pl.pallas_call(functools.partial(kernel, rows, d_model, q_heads, kv_heads...]
where the time goes in v6:
time: 27.5 us; the launch traced here: 27.4 us
  Pallas kernels  26.6 us (97%)
  between operations  0.8 us (3%)
    pallas_call x1, Pallas kernels, local_body(): pl.pallas_call(functools.partial(kernel, rows, d_model, q_heads, kv_heads...  25.4 us
    pallas_call x1, Pallas kernels, local_body(): pl.pallas_call(write_out, out_shape=(out, out), in_specs=[pl.BlockSpec(me...  1.2 us

profile of v6, /device:TPU:0, one launch (start us, length us, event | category | flops | bytes accessed | tf_op | source)
XLA Modules:
  0.0 27.4 jit_solution(5690056321505850017)
XLA Ops:
  0.6 25.4 %shard_map.77 = (bf16[256,1536]{1,0:T(8,128)(2,1)S(1)}, bf16[256,1536]{1,0:T(8,128)(2,1)S(1)}) custom-call(bf16[256,1536]{1,0:T(8,128)(2,1)} %x_hbm.1, bf16[256,1536]{1,0:T(8,128)(2,1)} %dy_hbm.1, bf16[1536,1536]{1,0:T(8,128)(2,1)} %wq_hbm.1, bf16[1536,256]{1,0:T(8,128)(2,1)} %wk_hbm.1, bf16[1536,256]{1,0:T(8,128)(2,1)} %wv_hbm.1, bf16[1536,1536]{1,0:T(8,128)(2,1)} %wo_hbm.1), custom_call_target="tpu_custom_call" | custom-call | tf_op jit(solution)/shard_map/pallas_call | solution.py:403
  26.0 1.2 %shard_map.78 = (bf16[256,1536]{1,0:T(8,128)(2,1)}, bf16[256,1536]{1,0:T(8,128)(2,1)}) custom-call(bf16[256,1536]{1,0:T(8,128)(2,1)S(1)} %get-tuple-element.4.y_v, bf16[256,1536]{1,0:T(8,128)(2,1)S(1)} %get-tuple-element.5.dx_v), custom_call_target="tpu_custom_call" | custom-call | tf_op jit(solution)/shard_map/pallas_call | solution.py:445

commit v7 on v6

--- a/solution.py
+++ b/solution.py
@@ -11,7 +11,7 @@
 HEAD_DIM = 128
 CHUNK = 128
 SPLIT = 128
-WRITES = 4
+WRITES = 1
 MESH = pl.DeviceIdType.MESH
 F32 = jnp.float32
 BF16 = jnp.bfloat16
@@ -190,6 +190,9 @@
         peers.reverse()
         pl.when(peers[0] != me)(f)
 
+    def stage_at(x):
+        return pl.when(me // 2 == x)
+
     def project_kv(w, kv_ref):
         out = mm(x_v[...], w[...]).astype(BF16)
         for h in range(kv_heads):
@@ -233,6 +236,10 @@
                 scores(i, 0)
                 scores(i, 1)
 
+    @stage_at(1)
+    def _():
+        forward(0)
+
     @stage
     def _():
         loads[5].wait()
@@ -243,12 +250,18 @@
             scores(group + n, 0)
             scores(group + n, 1)
 
-    @stage
+    def local_rest():
+        for i in second[n_pairs:]:
+            scores(i, 0)
+            scores(i, 1)
+
+    @stage_at(0)
     def _():
         forward(0)
-        for n in range(n_pairs):
-            scores(group + n_pairs + n, 0)
-            scores(group + n_pairs + n, 1)
+        local_rest()
+
+    @stage
+    def _():
         for n in first:
             scores(n, 2)
 
@@ -270,18 +283,33 @@
     @stage
     def _():
         loads[7].wait()
-        forward(1)
         forward(2)
         for n in range(n_pairs):
             project_do(n_pairs + n)
-            for i in (2 * n, 2 * n + 1):
-                finalize(i, (1, 0))
-                scores(group + i, 2)
+            finalize(2 * n, (1, 0))
+            finalize(2 * n + 1, (1, 0))
+
+    @stage_at(1)
+    def _():
+        local_rest()
+
+    @stage_at(1)
+    def _():
+        reduce_cross(0)
+
+    @stage
+    def _():
+        forward(1)
+        for i in second:
+            scores(i, 2)
         grads(0, 1, 2)
 
-    @stage
+    @stage_at(0)
     def _():
         reduce_cross(0)
+
+    @stage
+    def _():
         rs_copy(0, 1).start()
         ag_copy(2, 2).wait_recv()
         normalize_far(second, 1)

time: 27.5 us -> 27.8 us (1.011)
  Pallas kernels: 26.6 us -> 26.9 us
    pallas_call x1, Pallas kernels: 25.4 us -> 25.8 us  [local_body(): pl.pallas_call(functools.partial(kernel, rows, d_model, q_heads, kv_heads...]
where the time goes in v7:
time: 27.8 us; the launch traced here: 27.7 us
  Pallas kernels  26.9 us (97%)
  between operations  0.8 us (3%)
    pallas_call x1, Pallas kernels, local_body(): pl.pallas_call(functools.partial(kernel, rows, d_model, q_heads, kv_heads...  25.8 us
    pallas_call x1, Pallas kernels, local_body(): pl.pallas_call(write_out, out_shape=(out, out), in_specs=[pl.BlockSpec(me...  1.16 us

profile of v7, /device:TPU:0, one launch (start us, length us, event | category | flops | bytes accessed | tf_op | source)
XLA Modules:
  0.0 27.7 jit_solution(5201486883316613862)
XLA Ops:
  0.6 25.8 %shard_map.77 = (bf16[256,1536]{1,0:T(8,128)(2,1)S(1)}, bf16[256,1536]{1,0:T(8,128)(2,1)S(1)}) custom-call(bf16[256,1536]{1,0:T(8,128)(2,1)} %x_hbm.1, bf16[256,1536]{1,0:T(8,128)(2,1)} %dy_hbm.1, bf16[1536,1536]{1,0:T(8,128)(2,1)} %wq_hbm.1, bf16[1536,256]{1,0:T(8,128)(2,1)} %wk_hbm.1, bf16[1536,256]{1,0:T(8,128)(2,1)} %wv_hbm.1, bf16[1536,1536]{1,0:T(8,128)(2,1)} %wo_hbm.1), custom_call_target="tpu_custom_call" | custom-call | tf_op jit(solution)/shard_map/pallas_call | solution.py:431
  26.4 1.2 %shard_map.78 = (bf16[256,1536]{1,0:T(8,128)(2,1)}, bf16[256,1536]{1,0:T(8,128)(2,1)}) custom-call(bf16[256,1536]{1,0:T(8,128)(2,1)S(1)} %get-tuple-element.4.y_v, bf16[256,1536]{1,0:T(8,128)(2,1)S(1)} %get-tuple-element.5.dx_v), custom_call_target="tpu_custom_call" | custom-call | tf_op jit(solution)/shard_map/pallas_call | solution.py:473

commit v8 on v6

--- a/solution.py
+++ b/solution.py
@@ -11,7 +11,7 @@
 HEAD_DIM = 128
 CHUNK = 128
 SPLIT = 128
-WRITES = 4
+PIECES = 3
 MESH = pl.DeviceIdType.MESH
 F32 = jnp.float32
 BF16 = jnp.bfloat16
@@ -25,10 +25,10 @@
 
 def kernel(rows, d_model, q_heads, kv_heads,
            x_hbm, dy_hbm, wq_hbm, wk_hbm, wv_hbm, wo_hbm,
-           y_v, dx_v,
-           x_v, dy_v, wq_v, wk_v, wv_v, wo_v,
+           y_v, dx_acc, dk_v, wk_v,
+           x_v, dy_v, wq_v, wv_v, wo_v,
            qs, dot_v, k_all, v_all, kt, vt, pt, ds_t, e_buf, m_buf, l_buf, f_buf, o_v, dq_v,
-           part, recv_a, recv_b, recv_c, send_c, dx_acc,
+           part, recv_a, recv_b, recv_c, send_c,
            in_sem, ag_send, ag_recv, rs_send, rs_recv):
     group = q_heads // kv_heads
     d = HEAD_DIM
@@ -363,23 +363,21 @@
 
     @stage
     def _():
-        dk = own((2, 3), scale)
-        for n in range(d_model // 256):
-            cols = slice(n * 256, (n + 1) * 256)
-            dx_v[:, cols] = (dx_acc[:, cols] + mm(dk, wk_v[cols, :], NT)).astype(BF16)
+        dk_v[...] = own((2, 3), scale)
 
     pltpu.make_async_copy(dx_acc, dx_acc, rs_send).wait()
 
 
-def write_out(y_v, dx_v, y_hbm, dx_hbm, sem):
-    n = y_v.shape[0] // WRITES
-    copies = []
-    for i in range(WRITES):
-        part = slice(i * n, (i + 1) * n)
-        copies.append(pltpu.make_async_copy(dx_v.at[part], dx_hbm.at[part], sem.at[2 * i]))
-        copies.append(pltpu.make_async_copy(y_v.at[part], y_hbm.at[part], sem.at[2 * i + 1]))
-    for copy in copies:
+def finish(y_v, acc, dk, wk, y_hbm, dx_hbm, dx_v, sem):
+    copies = [pltpu.make_async_copy(y_v, y_hbm, sem.at[0])]
+    copies[0].start()
+    width = acc.shape[1] // PIECES
+    for n in range(PIECES):
+        cols = slice(n * width, (n + 1) * width)
+        dx_v[:, cols] = (acc[:, cols] + mm(dk[...], wk[cols, :], NT)).astype(BF16)
+        copy = pltpu.make_async_copy(dx_v.at[:, cols], dx_hbm.at[:, cols], sem.at[1 + n])
         copy.start()
+        copies.append(copy)
     for copy in copies:
         copy.wait()
 
@@ -400,16 +398,17 @@
         vmem = pl.BlockSpec(memory_space=pltpu.VMEM)
         out = jax.ShapeDtypeStruct((rows, d_model), BF16)
         items = 2 * kv_heads
-        y_v, dx_v = pl.pallas_call(
+        y_v, acc, dk, wk = pl.pallas_call(
             functools.partial(kernel, rows, d_model, q_heads, kv_heads),
-            out_shape=(out, out),
+            out_shape=(out, jax.ShapeDtypeStruct((rows, d_model), F32),
+                       jax.ShapeDtypeStruct((rows, kv_heads * d), BF16),
+                       jax.ShapeDtypeStruct((d_model, kv_heads * d), BF16)),
             in_specs=[hbm] * 6,
-            out_specs=(vmem, vmem),
+            out_specs=(vmem,) * 4,
             scratch_shapes=[
                 pltpu.VMEM((rows, d_model), BF16),
                 pltpu.VMEM((rows, d_model), BF16),
                 pltpu.VMEM((d_model, qw), BF16),
-                pltpu.VMEM((d_model, kv_heads * d), BF16),
                 pltpu.VMEM((d_model, kv_heads * d), BF16),
                 pltpu.VMEM((qw, d_model), BF16),
                 pltpu.VMEM((kv_heads, group * rows, d), BF16),
@@ -431,7 +430,6 @@
                 pltpu.VMEM((items, rows, d), F32),
                 pltpu.VMEM((items, rows, d), F32),
                 pltpu.VMEM((items, rows, d), F32),
-                pltpu.VMEM((rows, d_model), F32),
                 pltpu.SemaphoreType.DMA((8,)),
                 pltpu.SemaphoreType.DMA,
                 pltpu.SemaphoreType.DMA((items, 3)),
@@ -440,16 +438,17 @@
             ],
             compiler_params=pltpu.CompilerParams(
                 collective_id=0, has_side_effects=True,
-                vmem_limit_bytes=52 * 1024 * 1024),
+                vmem_limit_bytes=50 * 1024 * 1024),
         )(*(pltpu.with_memory_space_constraint(a, pltpu.HBM) for a in (x_loc, dy_loc, w_q, w_k, w_v, w_o)))
         return pl.pallas_call(
-            write_out,
+            finish,
             out_shape=(out, out),
-            in_specs=[pl.BlockSpec(memory_space=pl.ANY)] * 2,
+            in_specs=[vmem] * 4,
             out_specs=(hbm, hbm),
-            scratch_shapes=[pltpu.SemaphoreType.DMA((2 * WRITES,))],
-            compiler_params=pltpu.CompilerParams(vmem_limit_bytes=4 * 1024 * 1024),
-        )(y_v, dx_v)
+            scratch_shapes=[pltpu.VMEM((rows, d_model), BF16),
+                            pltpu.SemaphoreType.DMA((1 + PIECES,))],
+            compiler_params=pltpu.CompilerParams(vmem_limit_bytes=8 * 1024 * 1024),
+        )(y_v, acc, dk, wk)
 
     return jax.shard_map(local_body, mesh=mesh,
                          in_specs=(row_spec, row_spec, full_spec, full_spec, full_spec, full_spec),

time: 27.5 us -> 27.1 us (0.985)
  Pallas kernels: 26.6 us -> 26.2 us
    pallas_call x1, Pallas kernels: 25.4 us -> 25 us  [local_body(): pl.pallas_call(functools.partial(kernel, rows, d_model, q_heads, kv_heads...]
where the time goes in v8:
time: 27.1 us; the launch traced here: 27 us
  Pallas kernels  26.2 us (97%)
  between operations  0.8 us (3%)
    pallas_call x1, Pallas kernels, local_body(): pl.pallas_call(functools.partial(kernel, rows, d_model, q_heads, kv_heads...  25 us
    pallas_call x1, Pallas kernels, local_body(): pl.pallas_call(finish, out_shape=(out, out), in_specs=[vmem] * 4, out_spe...  1.18 us

profile of v8, /device:TPU:0, one launch (start us, length us, event | category | flops | bytes accessed | tf_op | source)
XLA Modules:
  0.0 27.0 jit_solution(15177237486797726868)
XLA Ops:
  0.6 25.0 %shard_map.77 = (bf16[256,1536]{1,0:T(8,128)(2,1)S(1)}, f32[256,1536]{1,0:T(8,128)S(1)}, bf16[256,256]{1,0:T(8,128)(2,1)S(1)}, bf16[1536,256]{1,0:T(8,128)(2,1)S(1)}) custom-call(bf16[256,1536]{1,0:T(8,128)(2,1)} %x_hbm.1, bf16[256,1536]{1,0:T(8,128)(2,1)} %dy_hbm.1, bf16[1536,1536]{1,0:T(8,128)(2,1)} %wq_hbm.1, bf16[1536,256]{1,0:T(8,128)(2,1)} %wk_hbm.1, ...), custom_call_target="tpu_custom_call" | custom-call | tf_op jit(solution)/shard_map/pallas_call | solution.py:401
  25.6 1.2 %shard_map.78 = (bf16[256,1536]{1,0:T(8,128)(2,1)}, bf16[256,1536]{1,0:T(8,128)(2,1)}) custom-call(bf16[256,1536]{1,0:T(8,128)(2,1)S(1)} %get-tuple-element.6.y_v, f32[256,1536]{1,0:T(8,128)S(1)} %get-tuple-element.7.acc, bf16[256,256]{1,0:T(8,128)(2,1)S(1)} %get-tuple-element.8.dk, bf16[1536,256]{1,0:T(8,128)(2,1)S(1)} %get-tuple-element.9.wk), custom_call_target="tpu_custom_call" | custom-call | tf_op jit(solution)/shard_map/pallas_call | solution.py:443

commit v9 on v8

--- a/solution.py
+++ b/solution.py
@@ -29,7 +29,7 @@
            x_v, dy_v, wq_v, wv_v, wo_v,
            qs, dot_v, k_all, v_all, kt, vt, pt, ds_t, e_buf, m_buf, l_buf, f_buf, o_v, dq_v,
            part, recv_a, recv_b, recv_c, send_c,
-           in_sem, ag_send, ag_recv, rs_send, rs_recv):
+           in_sem, ag_send, far_send, ag_recv, rs_send, rs_recv):
     group = q_heads // kv_heads
     d = HEAD_DIM
     n_keys = 4 * rows
@@ -41,9 +41,10 @@
     core = lax.rem(me, 2)
     partner = me + 1 - 2 * core
     cross = lax.rem(me + 2, 4)
+    far = lax.rem(partner + 2, 4)
 
     barrier = pltpu.get_barrier_semaphore()
-    for peer in (partner, cross):
+    for peer in (partner, cross, far):
         pl.semaphore_signal(barrier, inc=1, device_id={"cp": peer}, device_id_type=MESH)
 
     qcols = q_heads * d // 2
@@ -73,9 +74,21 @@
             send_sem=ag_send, recv_sem=ag_recv.at[i, hop],
             device_id={"cp": peer}, device_id_type=MESH)
 
+    def first_copy(src, peer):
+        return pltpu.make_async_remote_copy(
+            src_ref=slot(0, src), dst_ref=slot(0, 3),
+            send_sem=far_send, recv_sem=ag_recv.at[0, 2],
+            device_id={"cp": peer}, device_id_type=MESH)
+
     def forward(i):
         ag_copy(i, 1).wait_recv()
-        ag_copy(i, 2).start()
+        if i > 0:
+            ag_copy(i, 2).start()
+            return
+
+        @pl.when(me < 2)
+        def _():
+            first_copy(2, partner).start()
 
     def transpose_item(i, ref):
         for s in range(4):
@@ -199,6 +212,10 @@
         for h in range(kv_heads):
             i = 2 * h + item_of_head
             ag_copy(i, 1).start()
+            if i == 0:
+                @pl.when(me < 2)
+                def _():
+                    first_copy(0, far).start()
             ag_copy(i, 0).start()
 
     @stage
@@ -207,7 +224,7 @@
         loads[1].wait()
         project_kv(wk_v, k_all)
 
-    pl.semaphore_wait(barrier, 2)
+    pl.semaphore_wait(barrier, 3)
     send_kv(0)
 
     @stage
@@ -359,7 +376,13 @@
             cols = slice(n * 256, (n + 1) * 256)
             dx_acc[:, cols] = mm(dq_v[...], wq_v[cols, :], NT) + mm(dv, wv_v[cols, :], NT)
 
-    pltpu.make_async_copy(x_v, x_v, ag_send).wait()
+    sent = wv_v.at[pl.ds(0, (6 * kv_heads - 1) * rows * d // wv_v.shape[1])]
+    pltpu.make_async_copy(sent, sent, ag_send).wait()
+
+    @pl.when(me < 2)
+    def _():
+        both = k_all.at[0, pl.ds(0, 2 * rows)]
+        pltpu.make_async_copy(both, both, far_send).wait()
 
     @stage
     def _():
@@ -432,6 +455,7 @@
                 pltpu.VMEM((items, rows, d), F32),
                 pltpu.SemaphoreType.DMA((8,)),
                 pltpu.SemaphoreType.DMA,
+                pltpu.SemaphoreType.DMA,
                 pltpu.SemaphoreType.DMA((items, 3)),
                 pltpu.SemaphoreType.DMA,
                 pltpu.SemaphoreType.DMA((items, 3)),

time: 27.1 us -> 28.1 us (1.037)
  Pallas kernels: 26.2 us -> 27.2 us
    pallas_call x1, Pallas kernels: 25 us -> 26.1 us  [local_body(): pl.pallas_call(functools.partial(kernel, rows, d_model, q_heads, kv_heads...]
where the time goes in v9:
time: 28.1 us; the launch traced here: 28 us
  Pallas kernels  27.2 us (97%)
  between operations  0.8 us (3%)
    pallas_call x1, Pallas kernels, local_body(): pl.pallas_call(functools.partial(kernel, rows, d_model, q_heads, kv_heads...  26.1 us
    pallas_call x1, Pallas kernels, local_body(): pl.pallas_call(finish, out_shape=(out, out), in_specs=[vmem] * 4, out_spe...  1.18 us

profile of v9, /device:TPU:0, one launch (start us, length us, event | category | flops | bytes accessed | tf_op | source)
XLA Modules:
  0.0 28.0 jit_solution(17557139236748878741)
XLA Ops:
  0.6 26.1 %shard_map.77 = (bf16[256,1536]{1,0:T(8,128)(2,1)S(1)}, f32[256,1536]{1,0:T(8,128)S(1)}, bf16[256,256]{1,0:T(8,128)(2,1)S(1)}, bf16[1536,256]{1,0:T(8,128)(2,1)S(1)}) custom-call(bf16[256,1536]{1,0:T(8,128)(2,1)} %x_hbm.1, bf16[256,1536]{1,0:T(8,128)(2,1)} %dy_hbm.1, bf16[1536,1536]{1,0:T(8,128)(2,1)} %wq_hbm.1, bf16[1536,256]{1,0:T(8,128)(2,1)} %wk_hbm.1, ...), custom_call_target="tpu_custom_call" | custom-call | tf_op jit(solution)/shard_map/pallas_call | solution.py:424
  26.7 1.2 %shard_map.78 = (bf16[256,1536]{1,0:T(8,128)(2,1)}, bf16[256,1536]{1,0:T(8,128)(2,1)}) custom-call(bf16[256,1536]{1,0:T(8,128)(2,1)S(1)} %get-tuple-element.6.y_v, f32[256,1536]{1,0:T(8,128)S(1)} %get-tuple-element.7.acc, bf16[256,256]{1,0:T(8,128)(2,1)S(1)} %get-tuple-element.8.dk, bf16[1536,256]{1,0:T(8,128)(2,1)S(1)} %get-tuple-element.9.wk), custom_call_target="tpu_custom_call" | custom-call | tf_op jit(solution)/shard_map/pallas_call | solution.py:467

commit v10 on v8

--- a/solution.py
+++ b/solution.py
@@ -252,10 +252,13 @@
         for n in first:
             scores(n, 2)
 
-    def normalize_far(heads, r):
-        for i in heads:
+    def normalize_far(heads, r, filler=None):
+        if filler is not None:
+            for n in range(n_pairs):
+                filler(n)
+        for k, i in enumerate(heads):
             scores(i, 3)
-            if i > heads[0]:
+            if k > 0:
                 finalize(i - 1, (3, 2))
         finalize(heads[-1], (3, 2))
         grads(r, 3, 4)
@@ -269,22 +272,20 @@
 
     @stage
     def _():
-        loads[7].wait()
-        forward(1)
         forward(2)
-        for n in range(n_pairs):
-            project_do(n_pairs + n)
-            for i in (2 * n, 2 * n + 1):
-                finalize(i, (1, 0))
-                scores(group + i, 2)
+        for n in first:
+            finalize(n, (1, 0))
+            scores(group + n, 2)
         grads(0, 1, 2)
 
     @stage
     def _():
         reduce_cross(0)
         rs_copy(0, 1).start()
+        forward(1)
+        loads[7].wait()
         ag_copy(2, 2).wait_recv()
-        normalize_far(second, 1)
+        normalize_far(second, 1, lambda n: project_do(n_pairs + n))
 
     @stage
     def _():

time: 27.1 us -> 26.8 us (0.989)
  Pallas kernels: 26.2 us -> 25.9 us
    pallas_call x1, Pallas kernels: 25 us -> 24.7 us  [local_body(): pl.pallas_call(functools.partial(kernel, rows, d_model, q_heads, kv_heads...]
where the time goes in v10:
time: 26.8 us; the launch traced here: 26.7 us
  Pallas kernels  25.9 us (97%)
  between operations  0.8 us (3%)
    pallas_call x1, Pallas kernels, local_body(): pl.pallas_call(functools.partial(kernel, rows, d_model, q_heads, kv_heads...  24.7 us
    pallas_call x1, Pallas kernels, local_body(): pl.pallas_call(finish, out_shape=(out, out), in_specs=[vmem] * 4, out_spe...  1.18 us

profile of v10, /device:TPU:0, one launch (start us, length us, event | category | flops | bytes accessed | tf_op | source)
XLA Modules:
  0.0 26.7 jit_solution(13098391632197913295)
XLA Ops:
  0.6 24.7 %shard_map.77 = (bf16[256,1536]{1,0:T(8,128)(2,1)S(1)}, f32[256,1536]{1,0:T(8,128)S(1)}, bf16[256,256]{1,0:T(8,128)(2,1)S(1)}, bf16[1536,256]{1,0:T(8,128)(2,1)S(1)}) custom-call(bf16[256,1536]{1,0:T(8,128)(2,1)} %x_hbm.1, bf16[256,1536]{1,0:T(8,128)(2,1)} %dy_hbm.1, bf16[1536,1536]{1,0:T(8,128)(2,1)} %wq_hbm.1, bf16[1536,256]{1,0:T(8,128)(2,1)} %wk_hbm.1, ...), custom_call_target="tpu_custom_call" | custom-call | tf_op jit(solution)/shard_map/pallas_call | solution.py:402
  25.3 1.2 %shard_map.78 = (bf16[256,1536]{1,0:T(8,128)(2,1)}, bf16[256,1536]{1,0:T(8,128)(2,1)}) custom-call(bf16[256,1536]{1,0:T(8,128)(2,1)S(1)} %get-tuple-element.6.y_v, f32[256,1536]{1,0:T(8,128)S(1)} %get-tuple-element.7.acc, bf16[256,256]{1,0:T(8,128)(2,1)S(1)} %get-tuple-element.8.dk, bf16[1536,256]{1,0:T(8,128)(2,1)S(1)} %get-tuple-element.9.wk), custom_call_target="tpu_custom_call" | custom-call | tf_op jit(solution)/shard_map/pallas_call | solution.py:444

commit v11 on v10

--- a/solution.py
+++ b/solution.py
@@ -240,15 +240,13 @@
         ag_copy(2, 0).wait_recv()
         for n in range(n_pairs):
             project_do(n)
-            scores(group + n, 0)
-            scores(group + n, 1)
 
     @stage
     def _():
         forward(0)
-        for n in range(n_pairs):
-            scores(group + n_pairs + n, 0)
-            scores(group + n_pairs + n, 1)
+        for i in second:
+            scores(i, 0)
+            scores(i, 1)
         for n in first:
             scores(n, 2)
 

time: 26.8 us -> 26.8 us (level)
  no operation moved by 1% of the time
where the time goes in v11:
time: 26.8 us; the launch traced here: 26.7 us
  Pallas kernels  25.9 us (97%)
  between operations  0.8 us (3%)
    pallas_call x1, Pallas kernels, local_body(): pl.pallas_call(functools.partial(kernel, rows, d_model, q_heads, kv_heads...  24.8 us
    pallas_call x1, Pallas kernels, local_body(): pl.pallas_call(finish, out_shape=(out, out), in_specs=[vmem] * 4, out_spe...  1.18 us

profile of v11, /device:TPU:0, one launch (start us, length us, event | category | flops | bytes accessed | tf_op | source)
XLA Modules:
  0.0 26.7 jit_solution(1014140319150214039)
XLA Ops:
  0.6 24.8 %shard_map.77 = (bf16[256,1536]{1,0:T(8,128)(2,1)S(1)}, f32[256,1536]{1,0:T(8,128)S(1)}, bf16[256,256]{1,0:T(8,128)(2,1)S(1)}, bf16[1536,256]{1,0:T(8,128)(2,1)S(1)}) custom-call(bf16[256,1536]{1,0:T(8,128)(2,1)} %x_hbm.1, bf16[256,1536]{1,0:T(8,128)(2,1)} %dy_hbm.1, bf16[1536,1536]{1,0:T(8,128)(2,1)} %wq_hbm.1, bf16[1536,256]{1,0:T(8,128)(2,1)} %wk_hbm.1, ...), custom_call_target="tpu_custom_call" | custom-call | tf_op jit(solution)/shard_map/pallas_call | solution.py:400
  25.4 1.2 %shard_map.78 = (bf16[256,1536]{1,0:T(8,128)(2,1)}, bf16[256,1536]{1,0:T(8,128)(2,1)}) custom-call(bf16[256,1536]{1,0:T(8,128)(2,1)S(1)} %get-tuple-element.6.y_v, f32[256,1536]{1,0:T(8,128)S(1)} %get-tuple-element.7.acc, bf16[256,256]{1,0:T(8,128)(2,1)S(1)} %get-tuple-element.8.dk, bf16[1536,256]{1,0:T(8,128)(2,1)S(1)} %get-tuple-element.9.wk), custom_call_target="tpu_custom_call" | custom-call | tf_op jit(solution)/shard_map/pallas_call | solution.py:442
